TPU v7x, 32 devices: a whole 2x2x4 slice. The times are simulated.
32 devices in a mesh: dp: 4 (over x, core), tensor: 8 (over z, y).
Axes of the slice: x: 2, y: 2, z: 4, core: 2. Of those that a mesh axis runs over, the one named last changes fastest.
Arguments:
- out_grad: bfloat16 [2, 320, 4096], P(None, 'dp', 'tensor'), may hold values from -0.3125 to 0.3125
- layer_input: bfloat16 [2, 320, 4096], P(None, 'dp', 'tensor'), may hold values from -8 to 8
- w_down: bfloat16 [16384, 4096], P('tensor'), may hold values from -0.046875 to 0.046875
- silu_gate: bfloat16 [2, 320, 16384], P(None, 'dp', 'tensor'), may hold values from -6 to 6
- up_proj: bfloat16 [2, 320, 16384], P(None, 'dp', 'tensor'), may hold values from -6 to 6
- slope_codes: int32 [2, 32, 16384], P(None, 'dp', 'tensor'), may hold values from 0 to 1073741823
Outputs:
- grad_down: bfloat16 [16384, 4096], P('tensor', 'dp')
- grad_gate: bfloat16 [4096, 16384], P('dp', 'tensor')
- grad_up: bfloat16 [4096, 16384], P('dp', 'tensor')
Inputs may be any that keep to these rules, and one draw needn't show every extreme that they name: `slope_codes`: every word holds ten independent 3-bit codes; all eight codes occur.
All inputs are finite; a program needn't handle non-finite values.
Results may differ from a plain program's by a relative error of at most 0.018.
Values may be sent and summed in bfloat16 or wider, within the bound.
A program may use at most 128 MiB of HBM per device.

v0:
```python
import functools

import jax
import jax.numpy as jnp
import numpy as np
from jax import lax
from jax.experimental import pallas as pl
from jax.experimental.pallas import tpu as pltpu
from jax.sharding import PartitionSpec as P

SLOPE_LEVELS = (-0.09, 0.06, 0.22, 0.41, 0.6, 0.79, 0.96, 1.08)
MESH = pl.DeviceIdType.MESH
CHUNKS = 4


def exchange(n_dp, n_t, out_ref, in_ref, silu_ref, up_ref, code_ref, spread_ref, w_ref,
             xin, xout, hid_all, gate_all, up_all,
             og, wbuf, vbuf, own, stage,
             w_sem, p_send, p_recv, py_send, py_recv, og_sem,
             s_send, s_recv, h_send, h_sem, c_recv, zu_send, zd_send, y_send, y_recv,
             o_sem, o_send, o_recv, al_sem, ax_send, ax_recv, ac_send, ac_recv):
    chips = n_dp // 2
    rows = n_t // 2
    ratio = n_t // n_dp
    tokens, cols = out_ref.shape
    width = w_ref.shape[1]
    hidden = w_ref.shape[0]
    block = width // n_dp
    fc = hidden // CHUNKS
    units = 2 + 4 * (chips - 1)
    xg = (xin, xout)
    all_acts = (hid_all, gate_all, up_all)

    d = lax.axis_index("dp")
    t = lax.axis_index("tensor")
    q, c = d // 2, lax.rem(d, 2)
    z, y = t // 2, lax.rem(t, 2)
    partner = q * 2 + (1 - c)
    y_peer = z * 2 + (1 - y)
    owner = t // ratio
    owner_chip = owner // 2
    if ratio == 2:
        in_chain = d >= 0
        has_side = d >= 0
        chain_col, side_col = y, 1 - y
    else:
        in_chain = lax.rem(d, 2) == y
        has_side = lax.rem(d, 2) != y
        chain_col, side_col = y * 0, y * 0
    head_row = (d * ratio) // 2

    def chip_at(r):
        return lax.rem(q + r, chips) * 2 + c

    def row_at(k):
        return lax.rem(z + k, rows) * 2 + y

    def group_from(r, core):
        return lax.rem(q + chips - r, chips) * 2 + core

    def at_col(index, size):
        return pl.ds(pl.multiple_of(index * size, 128), size)

    def remote(src, dst, send, recv, dp, tensor):
        return pltpu.make_async_remote_copy(
            src_ref=src, dst_ref=dst, send_sem=send, recv_sem=recv,
            device_id={"dp": dp, "tensor": tensor}, device_id_type=MESH)

    barrier = pltpu.get_barrier_semaphore()
    greet = [(d, row_at(k)) for k in range(1, rows)] + [(d, y_peer), (partner, t)]
    greet += [(chip_at(r), t) for r in range(1, chips)]
    for dp, tensor in greet:
        pl.semaphore_signal(barrier, inc=1, device_id={"dp": dp, "tensor": tensor}, device_id_type=MESH)
    pl.semaphore_wait(barrier, len(greet))

    my_cols = og.at[:, at_col(t, cols)]

    def row_copy(k):
        return remote(out_ref, my_cols, p_send.at[k - 1], p_recv.at[k - 1], d, row_at(k))

    def row_wait(k):
        src = lax.rem(z + rows - k, rows) * 2 + y
        land = og.at[:, at_col(src, cols)]
        return remote(land, land, p_send.at[k - 1], p_recv.at[k - 1], d, y_peer)

    def side_copy(k):
        src = lax.rem(z + rows - k, rows) * 2 + y
        piece = og.at[:, at_col(src, cols)]
        return remote(out_ref if k == 0 else piece, piece, py_send.at[k], py_recv.at[k], d, y_peer)

    def side_wait(k):
        src = lax.rem(z + rows - k, rows) * 2 + (1 - y)
        piece = og.at[:, at_col(src, cols)]
        return remote(piece, piece, py_send.at[k], py_recv.at[k], d, y_peer)

    for k in range(1, rows):
        row_copy(k).start()
    side_copy(0).start()
    og_own = pltpu.make_async_copy(out_ref, my_cols, og_sem)
    og_own.start()

    away = owner_chip != q
    dist = lax.rem(owner_chip + chips - q, chips)
    slot = lax.max(dist - 1, 0)
    far = owner_chip * 2 + c

    def cross(a):
        src = in_ref if a == 0 else out_ref
        return remote(src, stage.at[a, slot], s_send.at[a], s_recv.at[a, slot], far, t)

    @pl.when(away)
    def _():
        for a in range(2):
            cross(a).start()

    def w_copy(j):
        part = pl.ds(pl.multiple_of(j * fc, 128), fc)
        return pltpu.make_async_copy(w_ref.at[part], wbuf.at[part], w_sem.at[j])

    for j in range(CHUNKS):
        w_copy(j).start()

    def unit_of(r, a):
        return 0 if r == 0 else 2 + (r - 1) * 4 + a * 2

    def hand(r, a, to_self):
        src = in_ref if r == 0 else stage.at[a, r - 1]
        u = unit_of(r, a) + c
        i = 0 if r == 0 else 1 + (r - 1) * 2 + a
        dst = xg[a].at[group_from(r, c), :, at_col(chain_col if ratio == 2 else 0, cols)]
        if to_self:
            return pltpu.make_async_copy(src, dst, c_recv.at[u])
        return remote(src, dst, h_send.at[i], c_recv.at[u], partner, t)

    source = owner_chip == q
    self_head = jnp.logical_and(source, owner == d)
    other_head = jnp.logical_and(source, owner != d)

    def hand_start(r, a):
        @pl.when(self_head)
        def _():
            hand(r, a, True).start()

        @pl.when(other_head)
        def _():
            hand(r, a, False).start()

    hand_start(0, 0)

    def f_part(j):
        return pl.ds(pl.multiple_of(j * fc, 128), fc)

    def own_local(a, j):
        return pltpu.make_async_copy(
            own.at[a, :, f_part(j)], all_acts[a].at[d, :, f_part(j)], al_sem.at[a, j])

    def own_chip(a, j, r):
        return remote(own.at[a, :, f_part(j)], all_acts[a].at[d, :, f_part(j)],
                      ax_send.at[a, r - 1, j], ax_recv.at[a, r - 1, j], chip_at(r), t)

    def own_core(a, j):
        return remote(own.at[a, :, f_part(j)], all_acts[a].at[d, :, f_part(j)],
                      ac_send.at[a, 0, j], ac_recv.at[a, 0, j], partner, t)

    def pass_core(a, j, r):
        land = all_acts[a].at[group_from(r, c), :, f_part(j)]
        return remote(land, land, ac_send.at[a, r, j], ac_recv.at[a, r, j], partner, t)

    def chip_wait(a, j, r):
        land = all_acts[a].at[group_from(r, c), :, f_part(j)]
        return remote(land, land, ax_send.at[a, r - 1, j], ax_recv.at[a, r - 1, j], partner, t)

    def core_wait(a, j, r):
        land = all_acts[a].at[group_from(r, 1 - c), :, f_part(j)]
        return remote(land, land, ac_send.at[a, r, j], ac_recv.at[a, r, j], partner, t)

    def send_own(a, j):
        for r in range(1, chips):
            own_chip(a, j, r).start()
        own_core(a, j).start()
        own_local(a, j).start()

    def early(j, carry):
        f = f_part(j)
        up_value = up_ref[:, f].astype(jnp.float32)
        own[0, :, f] = (silu_ref[:, f].astype(jnp.float32) * up_value).astype(jnp.bfloat16)
        words = code_ref[:, f]
        pieces = jnp.concatenate(
            [((words >> (3 * k)) & 7).astype(jnp.float32).astype(jnp.bfloat16) for k in range(10)], axis=0)
        symbols = jnp.dot(spread_ref[...], pieces, preferred_element_type=jnp.float32)
        slopes = jnp.full(symbols.shape, SLOPE_LEVELS[0], jnp.float32)
        for s in range(1, 8):
            slopes = jnp.where(symbols > s - 0.5, jnp.float32(SLOPE_LEVELS[s]), slopes)
        vbuf[:, f] = up_value * slopes
        send_own(0, j)
        return carry

    lax.fori_loop(0, CHUNKS, early, 0)

    for k in range(1, rows):
        row_wait(k).wait_recv()
        side_copy(k).start()

    for a in range(2):
        for r in range(1, chips):
            @pl.when(source)
            def _():
                land = stage.at[a, r - 1]
                remote(land, land, s_send.at[a], s_recv.at[a, r - 1], partner, t).wait_recv()
            hand_start(r, a)

    go_up = jnp.logical_and(in_chain, jnp.logical_and(z >= head_row, z + 1 < rows))
    go_down = jnp.logical_and(in_chain, jnp.logical_and(z <= head_row, z > 0))
    z_up = lax.min(z + 1, rows - 1) * 2 + y
    z_down = lax.max(z - 1, 0) * 2 + y

    def unit_ref(u, col):
        r, a, core = (0, 0, u) if u < 2 else ((u - 2) // 4 + 1, (u - 2) // 2 % 2, u % 2)
        return xg[a].at[group_from(r, core), :, at_col(col, cols)]

    def chain(u):
        piece = unit_ref(u, chain_col)
        return (remote(piece, piece, zu_send.at[u], c_recv.at[u], d, z_up),
                remote(piece, piece, zd_send.at[u], c_recv.at[u], d, z_down),
                remote(piece, piece, y_send.at[u], y_recv.at[u], d, y_peer))

    at_head = jnp.logical_and(in_chain, z == head_row)
    past_head = jnp.logical_and(in_chain, z != head_row)

    def chain_step(u, role):
        up_copy, down_copy, across = chain(u)

        @pl.when(role)
        def _():
            up_copy.wait_recv()

        @pl.when(jnp.logical_and(role, go_up))
        def _():
            up_copy.start()

        @pl.when(jnp.logical_and(role, go_down))
        def _():
            down_copy.start()

        @pl.when(role)
        def _():
            across.start()

    per = -(-units // CHUNKS)

    for u in range(units):
        chain_step(u, at_head)

    og_own.wait()
    for k in range(rows):
        side_wait(k).wait_recv()

    o_own = pltpu.make_async_copy(og.at[:, at_col(d, block)], xg[1].at[d], o_sem)
    o_own.start()
    o_other = remote(og.at[:, at_col(partner, block)], xg[1].at[d], o_send, o_recv, partner, t)
    o_other.start()

    def late(j, carry):
        f = f_part(j)
        w_copy(j).wait()
        grad = lax.dot_general(og[...], wbuf[f, :], (((1,), (1,)), ((), ())),
                               preferred_element_type=jnp.float32)
        own[1, :, f] = (grad * vbuf[:, f]).astype(jnp.bfloat16)
        own[2, :, f] = (grad * silu_ref[:, f].astype(jnp.float32)).astype(jnp.bfloat16)
        send_own(1, j)
        send_own(2, j)
        return carry

    lax.fori_loop(0, CHUNKS, late, 0)

    def relay(a):
        def step(j, carry):
            for r in range(1, chips):
                chip_wait(a, j, r).wait_recv()
                pass_core(a, j, r).start()
            return carry
        return step

    lax.fori_loop(0, CHUNKS, relay(0), 0)

    def relay_late(j, carry):
        relay(1)(j, carry)
        return relay(2)(j, carry)

    for j in range(CHUNKS):
        for u in range(j * per, min((j + 1) * per, units)):
            chain_step(u, past_head)
        relay_late(j, 0)

    for k in range(1, rows):
        row_copy(k).wait_send()
    for k in range(rows):
        side_copy(k).wait_send()

    @pl.when(away)
    def _():
        for a in range(2):
            cross(a).wait_send()

    @pl.when(other_head)
    def _():
        for r in range(chips):
            for a in range(2):
                if r or not a:
                    hand(r, a, False).wait_send()

    o_own.wait()
    o_other.wait()

    def unit_end(u):
        up_copy, down_copy, across = chain(u)

        @pl.when(go_up)
        def _():
            up_copy.wait_send()

        @pl.when(go_down)
        def _():
            down_copy.wait_send()

        @pl.when(in_chain)
        def _():
            across.wait_send()

        @pl.when(has_side)
        def _():
            piece = unit_ref(u, side_col)
            remote(piece, piece, y_send.at[u], y_recv.at[u], d, y_peer).wait_recv()

    for u in range(units):
        unit_end(u)

    def act_end(j, carry):
        for a in range(3):
            own_local(a, j).wait()
            own_core(a, j).wait_send()
            core_wait(a, j, 0).wait_recv()
            for r in range(1, chips):
                own_chip(a, j, r).wait_send()
                pass_core(a, j, r).wait_send()
                core_wait(a, j, r).wait_recv()
        return carry

    lax.fori_loop(0, CHUNKS, act_end, 0)


def products(in_ref, out_ref, hid_ref, gate_ref, up_ref, down_grad, gate_grad, up_grad, turned):
    @pl.when(pl.program_id(0) == 0)
    def _():
        turned[...] = in_ref[...].T

    def product(left, right):
        return jnp.dot(left, right, preferred_element_type=jnp.float32).astype(jnp.bfloat16)

    gate_grad[...] = product(turned[...], gate_ref[...])
    up_grad[...] = product(turned[...], up_ref[...])
    down_grad[...] = product(hid_ref[...].T, out_ref[...])


def shards(n_dp, n_t, out_grad, layer_input, w_down, silu_gate, up_proj, slope_codes):
    hidden, width = w_down.shape
    cols = out_grad.shape[2]
    tokens = out_grad.shape[0] * out_grad.shape[1]
    chips, rows, block = n_dp // 2, n_t // 2, width // n_dp
    words = tokens // 10
    row, col = np.arange(tokens)[:, None], np.arange(tokens)[None, :]
    spread = jnp.asarray(col == (row % 10) * words + row // 10, jnp.bfloat16)
    units = 2 + 4 * (chips - 1)
    far = chips - 1
    bf16 = jnp.bfloat16
    dma = pltpu.SemaphoreType.DMA
    vmem = pl.BlockSpec(memory_space=pltpu.VMEM)
    anywhere = pl.BlockSpec(memory_space=pl.ANY)
    acts = jax.ShapeDtypeStruct((n_dp, tokens, hidden), bf16)
    rows_of_block = jax.ShapeDtypeStruct((n_dp, tokens, block), bf16)
    flops = 2 * tokens * hidden * width
    xin, xout, hid, gate, up = pl.pallas_call(
        functools.partial(exchange, n_dp, n_t),
        out_shape=(rows_of_block, rows_of_block, acts, acts, acts),
        in_specs=[vmem] * 6 + [anywhere],
        out_specs=[anywhere] * 5,
        scratch_shapes=[
            pltpu.VMEM((tokens, width), bf16),
            pltpu.VMEM((hidden, width), bf16),
            pltpu.VMEM((tokens, hidden), jnp.float32),
            pltpu.VMEM((3, tokens, hidden), bf16),
            pltpu.VMEM((2, far, tokens, cols), bf16),
            dma((CHUNKS,)),
            dma((rows - 1,)), dma((rows - 1,)), dma((rows,)), dma((rows,)), dma,
            dma((2,)), dma((2, far)), dma((1 + 2 * far,)), dma,
            dma((units,)), dma((units,)), dma((units,)), dma((units,)), dma((units,)),
            dma, dma, dma,
            dma((3, CHUNKS)), dma((3, far, CHUNKS)), dma((3, far, CHUNKS)),
            dma((3, chips, CHUNKS)), dma((3, chips, CHUNKS)),
        ],
        compiler_params=pltpu.CompilerParams(
            collective_id=0, has_side_effects=True, vmem_limit_bytes=60 * 1024 * 1024),
        cost_estimate=pl.CostEstimate(flops=flops, bytes_accessed=50_000_000, transcendentals=0),
    )(
        out_grad.reshape(tokens, cols), layer_input.reshape(tokens, cols),
        silu_gate.reshape(tokens, hidden), up_proj.reshape(tokens, hidden),
        slope_codes.reshape(words, hidden), spread, w_down,
    )
    total = n_dp * tokens
    inputs, outputs = xin.reshape(total, block), xout.reshape(total, block)
    piece = min(512, hidden)
    whole = pl.BlockSpec((total, block), lambda i: (0, 0))
    part = pl.BlockSpec((total, piece), lambda i: (0, i))
    tall = pl.BlockSpec((block, piece), lambda i: (0, i))
    across = jax.ShapeDtypeStruct((block, hidden), bf16)
    return pl.pallas_call(
        products,
        grid=(hidden // piece,),
        out_shape=(jax.ShapeDtypeStruct((hidden, block), bf16), across, across),
        in_specs=[whole, whole, part, part, part],
        out_specs=[pl.BlockSpec((piece, block), lambda i: (i, 0)), tall, tall],
        scratch_shapes=[pltpu.VMEM((block, total), bf16)],
        compiler_params=pltpu.CompilerParams(vmem_limit_bytes=60 * 1024 * 1024),
    )(
        inputs, outputs, hid.reshape(total, hidden),
        gate.reshape(total, hidden), up.reshape(total, hidden),
    )


def solution(mesh):
    n_dp, n_t = mesh.shape["dp"], mesh.shape["tensor"]
    return jax.shard_map(
        functools.partial(shards, n_dp, n_t),
        mesh=mesh,
        in_specs=(
            P(None, "dp", "tensor"),
            P(None, "dp", "tensor"),
            P("tensor", None),
            P(None, "dp", "tensor"),
            P(None, "dp", "tensor"),
            P(None, "dp", "tensor"),
        ),
        out_specs=(P("tensor", "dp"), P("dp", "tensor"), P("dp", "tensor")),
        check_vma=False,
    )
```

profile of v0, /device:TPU:3, one launch (start us, length us, event | category | flops | bytes accessed | tf_op | source)
XLA Modules:
  0.0 77.1 jit_solution(5870915271707755844)
XLA Ops:
  0.6 62.0 %shard_map.94 = (bf16[4,160,1024]{2,1,0:T(8,128)(2,1)}, bf16[4,160,1024]{2,1,0:T(8,128)(2,1)}, bf16[4,160,2048]{2,1,0:T(8,128)(2,1)}, bf16[4,160,2048]{2,1,0:T(8,128)(2,1)}, bf16[4,160,2048]{2,1,0:T(8,128)(2,1)}) custom-call(bf16[160,512]{1,0:T(8,128)(2,1)} %bitcast.17, bf16[160,512]{1,0:T(8,128)(2,1)} %bitcast.18, bf16[160,2048]{1,0:T(8,128)(2,1)} %bitcast.15, ...), custom_call_target="tpu_custom_call" | custom-call | flops 2684354560 | bytes 50000000 | tf_op jit(solution)/shard_map/pallas_call | solution.py:382
  62.6 14.5 %shard_map.95 = (bf16[2048,1024]{1,0:T(8,128)(2,1)}, bf16[1024,2048]{1,0:T(8,128)(2,1)}, bf16[1024,2048]{1,0:T(8,128)(2,1)}) custom-call(bf16[640,1024]{1,0:T(8,128)(2,1)} %bitcast.13, bf16[640,1024]{1,0:T(8,128)(2,1)} %bitcast.14, bf16[640,2048]{1,0:T(8,128)(2,1)} %bitcast.10, bf16[640,2048]{1,0:T(8,128)(2,1)} %bitcast.11, bf16[640,2048]{1,0:T(8,128)(2,1)} %bitcast.12), custom_call_target="tpu_custom_call" | custom-call | tf_op jit(solution)/shard_map/pallas_call | solution.py:416
where the time goes:
time: 77.3 us; the launch traced here: 77.1 us
  Pallas kernels  76.5 us (99%)
    pallas_call x1, Pallas kernels, shards(): pl.pallas_call(functools.partial(exchange, n_dp, n_t), out_shape=(rows_of...  62 us
    pallas_call x1, Pallas kernels, shards(): pl.pallas_call(products, grid=(hidden // piece,), out_shape=(jax.ShapeDty...  14.5 us

commit v1 on v0

v1 whole, which is shorter than its diff:
```python
import functools

import jax
import jax.numpy as jnp
import numpy as np
from jax import lax
from jax.experimental import pallas as pl
from jax.experimental.pallas import tpu as pltpu
from jax.sharding import PartitionSpec as P

SLOPE_LEVELS = (-0.09, 0.06, 0.22, 0.41, 0.6, 0.79, 0.96, 1.08)
MESH = pl.DeviceIdType.MESH
EARLY = 4
HELD = 1
LATE = 8
TAIL = 2
SPLIT = 2
LAG = 3


def exchange(n_dp, n_t, out_hbm, in_hbm, silu_hbm, up_hbm, code_hbm, spread_hbm, w_hbm,
             down, gate_main, up_main, turned, gate_all, up_all,
             og, li, silu, up, codes, spread, w, slopes_up, acc, hid_all, xin, xout,
             l_sem, w_sem, u_send, u_recv, d_send, d_recv, y_send, y_recv,
             x_send, c_recv, zu_send, zd_send, cy_send, cy_recv, o_sem, o_send, o_recv,
             ax_send, ax_recv, ac_send, ac_recv):
    chips = n_dp // 2
    rows = n_t // 2
    ratio = n_t // n_dp
    tokens, cols = out_hbm.shape
    hidden, width = w_hbm.shape
    block = width // n_dp
    part = cols // SPLIT
    total = n_dp * tokens
    n_in, n_out = n_dp * SPLIT, (n_dp - 2) * SPLIT
    acts = (hid_all, gate_all, up_all)
    pieces = (EARLY, LATE, LATE)

    d = lax.axis_index("dp")
    t = lax.axis_index("tensor")
    q, c = d // 2, lax.rem(d, 2)
    z, y = t // 2, lax.rem(t, 2)
    partner = q * 2 + (1 - c)
    y_peer = z * 2 + (1 - y)
    z_up = lax.min(z + 1, rows - 1) * 2 + y
    z_down = lax.max(z - 1, 0) * 2 + y
    has_up, has_down = z + 1 < rows, z > 0
    owner = t // ratio
    if ratio == 2:
        in_chain = d >= 0
        has_side = d >= 0
        chain_col, side_col = y, 1 - y
    else:
        in_chain = lax.rem(d, 2) == y
        has_side = lax.rem(d, 2) != y
        chain_col, side_col = y * 0, y * 0
    in_head = (d * ratio) // 2
    out_head = lax.rem(in_head + rows // 2, rows)

    def chip_at(r):
        return lax.rem(q + r, chips) * 2 + c

    def group_from(r, core):
        return lax.rem(q + chips - r, chips) * 2 + core

    def span(index, size):
        return pl.ds(pl.multiple_of(index * size, 128), size)

    def remote(src, dst, send, recv, dp, tensor):
        return pltpu.make_async_remote_copy(
            src_ref=src, dst_ref=dst, send_sem=send, recv_sem=recv,
            device_id={"dp": dp, "tensor": tensor}, device_id_type=MESH)

    my_cols = og.at[:, span(t, cols)]
    loads = [
        pltpu.make_async_copy(out_hbm, my_cols, l_sem.at[0]),
        pltpu.make_async_copy(in_hbm, li, l_sem.at[1]),
        pltpu.make_async_copy(silu_hbm, silu, l_sem.at[2]),
        pltpu.make_async_copy(up_hbm, up, l_sem.at[3]),
        pltpu.make_async_copy(code_hbm, codes, l_sem.at[4]),
        pltpu.make_async_copy(spread_hbm, spread, l_sem.at[5]),
    ]
    for load in loads:
        load.start()

    fw = min(512, hidden)

    def w_copy(j):
        f = span(j, fw)
        return pltpu.make_async_copy(w_hbm.at[f], w.at[f], w_sem.at[j])

    for j in range(hidden // fw):
        w_copy(j).start()

    barrier = pltpu.get_barrier_semaphore()
    greet = [(d, y_peer), (partner, t)]
    greet += [(chip_at(r), t) for r in range(1, chips)]
    for r in range(1, chips):
        greet.append((lax.rem(q + r, chips) * 2 + 1 - c, t))
    for dp, tensor in greet:
        pl.semaphore_signal(barrier, inc=1, device_id={"dp": dp, "tensor": tensor}, device_id_type=MESH)

    @pl.when(has_up)
    def _():
        pl.semaphore_signal(barrier, inc=1, device_id={"dp": d, "tensor": z_up}, device_id_type=MESH)

    @pl.when(has_down)
    def _():
        pl.semaphore_signal(barrier, inc=1, device_id={"dp": d, "tensor": z_down}, device_id_type=MESH)

    pl.semaphore_wait(barrier, len(greet) + has_up.astype(jnp.int32) + has_down.astype(jnp.int32))

    def og_piece(row, col, h):
        return og.at[:, span((row * 2 + col) * SPLIT + h, part)]

    def up_copy(s, h):
        piece = og_piece(lax.max(z - s + 1, 0), y, h)
        return remote(piece, piece, u_send.at[s, h], u_recv.at[s, h], d, z_up)

    def down_copy(s, h):
        piece = og_piece(lax.min(z + s - 1, rows - 1), y, h)
        return remote(piece, piece, d_send.at[s, h], d_recv.at[s, h], d, z_down)

    def up_wait(s, h):
        piece = og_piece(lax.max(z - s, 0), y, h)
        return remote(piece, piece, u_send.at[s, h], u_recv.at[s, h], d, z_up)

    def down_wait(s, h):
        piece = og_piece(lax.min(z + s, rows - 1), y, h)
        return remote(piece, piece, d_send.at[s, h], d_recv.at[s, h], d, z_down)

    def across(row, h):
        piece = og_piece(row, y, h)
        return remote(piece, piece, y_send.at[row, h], y_recv.at[row, h], d, y_peer)

    def across_wait(row, h):
        piece = og_piece(row, 1 - y, h)
        return remote(piece, piece, y_send.at[row, h], y_recv.at[row, h], d, y_peer)

    loads[0].wait()
    for h in range(SPLIT):
        across(z, h).start()

        @pl.when(has_up)
        def _():
            up_copy(1, h).start()

        @pl.when(has_down)
        def _():
            down_copy(1, h).start()

    def in_piece(group, col, h):
        return xin.at[group, :, span(col * SPLIT + h, part)]

    def out_piece(group, col, h):
        return xout.at[group, :, span(col * SPLIT + h, part)]

    in_slot = (lax.rem(owner // 2 + chips - q, chips) * 2 + c) * SPLIT

    def li_remote(h):
        return remote(li.at[:, h * part:(h + 1) * part], in_piece(d, chain_col_of(t), h),
                      x_send.at[h], c_recv.at[in_slot + h], owner, t)

    def li_local(h):
        return pltpu.make_async_copy(li.at[:, h * part:(h + 1) * part], in_piece(d, chain_col_of(t), h),
                                     c_recv.at[in_slot + h])

    def chain_col_of(tensor):
        return lax.rem(tensor, 2) if ratio == 2 else tensor * 0

    loads[1].wait()
    owned = owner == d

    @pl.when(owned)
    def _():
        for h in range(SPLIT):
            li_local(h).start()

    @pl.when(jnp.logical_not(owned))
    def _():
        for h in range(SPLIT):
            li_remote(h).start()

    far_row = lax.rem(z + rows // 2, rows)
    far_owner = (far_row * 2 + y) // ratio
    crosses = far_owner // 2 != q
    far_dist = lax.max(lax.rem(far_owner // 2 + chips - q, chips), 1)
    out_slot = n_in + ((far_dist - 1) * 2 + c) * SPLIT

    def og_far(h):
        return remote(og_piece(far_row, y, h), out_piece(d, chain_col_of(t), h),
                      x_send.at[SPLIT + h], c_recv.at[out_slot + h], far_owner, t)

    def f_part(a, j):
        return span(j, hidden // pieces[a])

    def own_chip(a, j, r):
        own = acts[a].at[d, :, f_part(a, j)]
        return remote(own, own, ax_send.at[a, r - 1, j], ax_recv.at[a, r - 1, j], chip_at(r), t)

    def own_core(a, j):
        own = acts[a].at[d, :, f_part(a, j)]
        return remote(own, own, ac_send.at[a, 0, j], ac_recv.at[a, 0, j], partner, t)

    def pass_core(a, j, r):
        land = acts[a].at[group_from(r, c), :, f_part(a, j)]
        return remote(land, land, ac_send.at[a, r, j], ac_recv.at[a, r, j], partner, t)

    def chip_wait(a, j, r):
        land = acts[a].at[group_from(r, c), :, f_part(a, j)]
        return remote(land, land, ax_send.at[a, r - 1, j], ax_recv.at[a, r - 1, j], partner, t)

    def core_wait(a, j, r):
        land = acts[a].at[group_from(r, 1 - c), :, f_part(a, j)]
        return remote(land, land, ac_send.at[a, r, j], ac_recv.at[a, r, j], partner, t)

    def send_own(a, j):
        for r in range(1, chips):
            own_chip(a, j, r).start()
        own_core(a, j).start()

    def relay(a, j):
        for r in range(1, chips):
            chip_wait(a, j, r).wait_recv()
            pass_core(a, j, r).start()

    loads[2].wait()
    loads[3].wait()

    def early(j, carry):
        f = f_part(0, j)
        hid_all[d, :, f] = (silu[:, f].astype(jnp.float32) * up[:, f].astype(jnp.float32)).astype(jnp.bfloat16)

        @pl.when(j < EARLY - HELD)
        def _():
            send_own(0, j)
        return carry

    lax.fori_loop(0, EARLY, early, 0)

    loads[4].wait()
    loads[5].wait()
    acc[...] = jnp.zeros_like(acc)

    def decode(j, carry):
        f = span(j, fw)
        words = codes[:, f]
        symbols = jnp.dot(
            spread[...],
            jnp.concatenate([((words >> (3 * k)) & 7).astype(jnp.float32).astype(jnp.bfloat16) for k in range(10)], axis=0),
            preferred_element_type=jnp.float32)
        slopes = jnp.full(symbols.shape, SLOPE_LEVELS[0], jnp.float32)
        for s in range(1, 8):
            slopes = jnp.where(symbols > s - 0.5, jnp.float32(SLOPE_LEVELS[s]), slopes)
        slopes_up[:, f] = up[:, f].astype(jnp.float32) * slopes
        return carry

    lax.fori_loop(0, hidden // fw, decode, 0)

    def unit(i):
        h, u = lax.rem(i, SPLIT), i // SPLIT
        return lax.rem(u, 2), u // 2, h

    def in_ref(i, col):
        core, r, h = unit(i)
        return in_piece(group_from(r, core), col, h)

    def out_ref(i, col):
        core, r, h = unit(i)
        return out_piece(group_from(r + 1, core), col, h)

    def chain(i, base, ref):
        piece = ref(i, chain_col)
        n = base + i
        return (remote(piece, piece, zu_send.at[n], c_recv.at[n], d, z_up),
                remote(piece, piece, zd_send.at[n], c_recv.at[n], d, z_down),
                remote(piece, piece, cy_send.at[n], cy_recv.at[n], d, y_peer))

    def goes(head):
        return (jnp.logical_and(in_chain, jnp.logical_and(z >= head, has_up)),
                jnp.logical_and(in_chain, jnp.logical_and(z <= head, has_down)))

    def chain_step(i, base, ref, head):
        up_next, down_next, side = chain(i, base, ref)
        go_up, go_down = goes(head)
        up_next.wait_recv()

        @pl.when(go_up)
        def _():
            up_next.start()

        @pl.when(go_down)
        def _():
            down_next.start()

        side.start()

    in_far = lax.max(z - in_head, in_head - z)
    out_far = lax.max(z - out_head, out_head - z)
    at_in_head = jnp.logical_and(in_chain, in_far == 0)

    def matmul_piece(piece):
        k = span(piece, cols)

        def f_step(j, carry):
            f = span(j, fw)
            acc[:, f] += lax.dot_general(og[:, k], w[f, k], (((1,), (1,)), ((), ())),
                                         preferred_element_type=jnp.float32)
            return carry

        lax.fori_loop(0, hidden // fw, f_step, 0)

    def gather(s, carry):
        below, above = z >= s, z + s < rows
        for h in range(SPLIT):
            @pl.when(below)
            def _():
                up_wait(s, h).wait_recv()

                @pl.when(has_up)
                def _():
                    up_copy(s + 1, h).start()

                across(lax.max(z - s, 0), h).start()

            @pl.when(above)
            def _():
                down_wait(s, h).wait_recv()

                @pl.when(has_down)
                def _():
                    down_copy(s + 1, h).start()

                across(lax.min(z + s, rows - 1), h).start()

        @pl.when(s == rows // 2)
        def _():
            @pl.when(crosses)
            def _():
                for h in range(SPLIT):
                    og_far(h).start()

            for j in range(EARLY - HELD, EARLY):
                send_own(0, j)

        @pl.when(s == 1)
        def _():
            for j in range(hidden // fw):
                w_copy(j).wait()

        @pl.when(jnp.logical_and(s == rows - 1, at_in_head))
        def _():
            def start(i, carry):
                chain_step(i, 0, in_ref, in_head)
                return carry

            lax.fori_loop(0, n_in, start, 0)

        def piece_step(k, carry):
            side = k >= 3
            dist = jnp.where(k == 0, 0, jnp.where(side, s - 1, s))
            down_side = jnp.logical_or(k == 1, k == 3)
            row = jnp.where(down_side, z - dist, z + dist)
            wanted = jnp.where(k == 0, s == 1, jnp.logical_or(dist > 0, down_side))
            valid = jnp.logical_and(wanted, jnp.logical_and(row >= 0, row < rows))

            @pl.when(valid)
            def _():
                @pl.when(side)
                def _():
                    for h in range(SPLIT):
                        across_wait(row, h).wait_recv()

                matmul_piece(row * 2 + jnp.where(side, 1 - y, y))
            return carry

        lax.fori_loop(0, 5, piece_step, 0)
        return carry

    lax.fori_loop(1, rows + 1, gather, 0)

    o_own = pltpu.make_async_copy(og.at[:, span(d, block)], xout.at[d], o_sem)
    o_own.start()
    o_other = remote(og.at[:, span(partner, block)], xout.at[d], o_send, o_recv, partner, t)
    o_other.start()

    def late(j):
        f = f_part(1, j)
        grad = acc[:, f]
        gate_all[d, :, f] = (grad * slopes_up[:, f]).astype(jnp.bfloat16)
        up_all[d, :, f] = (grad * silu[:, f].astype(jnp.float32)).astype(jnp.bfloat16)
        send_own(1, j)
        send_own(2, j)

    steps = max(n_in + rows - 2, n_out + LAG + rows - 1, LATE)

    def wave(s, carry):
        @pl.when(s < LATE)
        def _():
            late(s)

        i = s - (in_far - 1)

        @pl.when(jnp.logical_and(jnp.logical_and(in_chain, in_far > 0), jnp.logical_and(i >= 0, i < n_in)))
        def _():
            chain_step(i, 0, in_ref, in_head)

        o = s - LAG - out_far

        @pl.when(jnp.logical_and(in_chain, jnp.logical_and(o >= 0, o < n_out)))
        def _():
            chain_step(o, n_in, out_ref, out_head)
        return carry

    lax.fori_loop(0, steps, wave, 0)

    def hidden_relay(j, carry):
        relay(0, j)
        return carry

    lax.fori_loop(0, EARLY, hidden_relay, 0)

    def side_wait(i, base, ref):
        @pl.when(has_side)
        def _():
            piece = ref(i, side_col)
            remote(piece, piece, cy_send.at[base + i], cy_recv.at[base + i], d, y_peer).wait_recv()

    def out_side(i, carry):
        side_wait(i, n_in, out_ref)
        return carry

    def in_side(i, carry):
        side_wait(i, 0, in_ref)
        return carry

    lax.fori_loop(0, n_out, out_side, 0)
    o_own.wait()
    o_other.wait()

    def from_partner(a):
        def step(j, carry):
            for r in range(chips):
                core_wait(a, j, r).wait_recv()
            return carry
        return step

    lax.fori_loop(0, EARLY, from_partner(0), 0)

    def product(left, right):
        return jnp.dot(left, right, preferred_element_type=jnp.float32).astype(jnp.bfloat16)

    def down_step(j, carry):
        f = span(j, fw)
        down[f, :] = product(hid_all[:, :, f].reshape(total, fw).T, xout[...].reshape(total, block))
        return carry

    lax.fori_loop(0, hidden // fw, down_step, 0)
    lax.fori_loop(0, n_in, in_side, 0)
    turned[...] = xin[...].reshape(total, block).T

    def main_step(j, carry):
        relay(1, j)
        relay(2, j)

        @pl.when(j > 0)
        def _():
            for a in (1, 2):
                from_partner(a)(j - 1, 0)
            f = f_part(1, j - 1)
            size = hidden // LATE
            gate_main[:, f] = product(turned[...], gate_all[:, :, f].reshape(total, size))
            up_main[:, f] = product(turned[...], up_all[:, :, f].reshape(total, size))
        return carry

    lax.fori_loop(0, LATE - TAIL + 1, main_step, 0)
    for j in range(LATE - TAIL + 1, LATE):
        relay(1, j)
        relay(2, j)

    def gather_end(s, carry):
        for h in range(SPLIT):
            @pl.when(jnp.logical_and(has_up, z >= s - 1))
            def _():
                up_copy(s, h).wait_send()

            @pl.when(jnp.logical_and(has_down, z + s - 1 < rows))
            def _():
                down_copy(s, h).wait_send()

            across(s - 1, h).wait_send()
        return carry

    lax.fori_loop(1, rows + 1, gather_end, 0)

    @pl.when(jnp.logical_not(owned))
    def _():
        for h in range(SPLIT):
            li_remote(h).wait_send()

    @pl.when(crosses)
    def _():
        for h in range(SPLIT):
            og_far(h).wait_send()

    def chain_end(i, base, ref, head):
        up_next, down_next, side = chain(i, base, ref)
        go_up, go_down = goes(head)

        @pl.when(go_up)
        def _():
            up_next.wait_send()

        @pl.when(go_down)
        def _():
            down_next.wait_send()

        @pl.when(in_chain)
        def _():
            side.wait_send()

    def in_end(i, carry):
        chain_end(i, 0, in_ref, in_head)
        return carry

    def out_end(i, carry):
        chain_end(i, n_in, out_ref, out_head)
        return carry

    lax.fori_loop(0, n_in, in_end, 0)
    lax.fori_loop(0, n_out, out_end, 0)

    def sent(a):
        def step(j, carry):
            own_core(a, j).wait_send()
            for r in range(1, chips):
                own_chip(a, j, r).wait_send()
                pass_core(a, j, r).wait_send()
            return carry
        return step

    for a in range(3):
        lax.fori_loop(0, pieces[a], sent(a), 0)
    for a in (1, 2):
        lax.fori_loop(LATE - TAIL, LATE, from_partner(a), 0)


def finish(down_in, gate_in, up_in, turned, gate_all, up_all, down_out, gate_out, up_out, gate_tail, up_tail, sems):
    n_dp, tokens, hidden = gate_all.shape
    total = n_dp * tokens
    main = gate_in.shape[1]
    size = (hidden - main) // TAIL
    copies = [
        pltpu.make_async_copy(down_in, down_out, sems.at[0]),
        pltpu.make_async_copy(gate_in, gate_out.at[:, :main], sems.at[1]),
        pltpu.make_async_copy(up_in, up_out.at[:, :main], sems.at[2]),
    ]
    for copy in copies:
        copy.start()
    for j in range(TAIL):
        f = slice(main + j * size, main + (j + 1) * size)
        for k, (acts, tail, out) in enumerate(((gate_all, gate_tail, gate_out), (up_all, up_tail, up_out))):
            tail[j] = jnp.dot(turned[...], acts[:, :, f].reshape(total, size),
                              preferred_element_type=jnp.float32).astype(jnp.bfloat16)
            copies.append(pltpu.make_async_copy(tail.at[j], out.at[:, f], sems.at[3 + j * 2 + k]))
            copies[-1].start()
    for copy in copies:
        copy.wait()


def shards(n_dp, n_t, out_grad, layer_input, w_down, silu_gate, up_proj, slope_codes):
    hidden, width = w_down.shape
    cols = out_grad.shape[2]
    tokens = out_grad.shape[0] * out_grad.shape[1]
    chips, rows, block = n_dp // 2, n_t // 2, width // n_dp
    words = tokens // 10
    total = n_dp * tokens
    row, col = np.arange(tokens)[:, None], np.arange(tokens)[None, :]
    spread = jnp.asarray(col == (row % 10) * words + row // 10, jnp.bfloat16)
    units = (2 * n_dp - 2) * SPLIT
    far = chips - 1
    bf16 = jnp.bfloat16
    dma = pltpu.SemaphoreType.DMA
    vmem = pl.BlockSpec(memory_space=pltpu.VMEM)
    anywhere = pl.BlockSpec(memory_space=pl.ANY)
    main = hidden // LATE * (LATE - TAIL)
    flops = 2 * tokens * hidden * width + 5 * total * hidden * block
    held = pl.pallas_call(
        functools.partial(exchange, n_dp, n_t),
        out_shape=tuple(pltpu.VMEM(shape, bf16) for shape in (
            (hidden, block), (block, main), (block, main), (block, total),
            (n_dp, tokens, hidden), (n_dp, tokens, hidden))),
        in_specs=[anywhere] * 7,
        out_specs=[vmem] * 6,
        scratch_shapes=[
            pltpu.VMEM((tokens, width), bf16),
            pltpu.VMEM((tokens, cols), bf16),
            pltpu.VMEM((tokens, hidden), bf16),
            pltpu.VMEM((tokens, hidden), bf16),
            pltpu.VMEM((words, hidden), jnp.int32),
            pltpu.VMEM((tokens, tokens), bf16),
            pltpu.VMEM((hidden, width), bf16),
            pltpu.VMEM((tokens, hidden), jnp.float32),
            pltpu.VMEM((tokens, hidden), jnp.float32),
            pltpu.VMEM((n_dp, tokens, hidden), bf16),
            pltpu.VMEM((n_dp, tokens, block), bf16),
            pltpu.VMEM((n_dp, tokens, block), bf16),
            dma((6,)), dma((max(1, hidden // min(512, hidden)),)),
            dma((rows + 2, SPLIT)), dma((rows + 2, SPLIT)), dma((rows + 2, SPLIT)), dma((rows + 2, SPLIT)),
            dma((rows, SPLIT)), dma((rows, SPLIT)),
            dma((2 * SPLIT,)), dma((units,)), dma((units,)), dma((units,)), dma((units,)), dma((units,)),
            dma, dma, dma,
            dma((3, far, LATE)), dma((3, far, LATE)), dma((3, chips, LATE)), dma((3, chips, LATE)),
        ],
        compiler_params=pltpu.CompilerParams(
            collective_id=0, has_side_effects=True, vmem_limit_bytes=38 * 1024 * 1024),
        cost_estimate=pl.CostEstimate(flops=flops, bytes_accessed=20_000_000, transcendentals=0),
    )(
        out_grad.reshape(tokens, cols), layer_input.reshape(tokens, cols),
        silu_gate.reshape(tokens, hidden), up_proj.reshape(tokens, hidden),
        slope_codes.reshape(words, hidden), spread, w_down,
    )
    across = jax.ShapeDtypeStruct((block, hidden), bf16)
    size = hidden // LATE
    return pl.pallas_call(
        finish,
        out_shape=(jax.ShapeDtypeStruct((hidden, block), bf16), across, across),
        in_specs=[vmem] * 6,
        out_specs=[anywhere] * 3,
        scratch_shapes=[
            pltpu.VMEM((TAIL, block, size), bf16), pltpu.VMEM((TAIL, block, size), bf16), dma((3 + 2 * TAIL,))],
        compiler_params=pltpu.CompilerParams(vmem_limit_bytes=12 * 1024 * 1024),
    )(*(pltpu.with_memory_space_constraint(value, pltpu.VMEM) for value in held))


def solution(mesh):
    n_dp, n_t = mesh.shape["dp"], mesh.shape["tensor"]
    return jax.shard_map(
        functools.partial(shards, n_dp, n_t),
        mesh=mesh,
        in_specs=(
            P(None, "dp", "tensor"),
            P(None, "dp", "tensor"),
            P("tensor", None),
            P(None, "dp", "tensor"),
            P(None, "dp", "tensor"),
            P(None, "dp", "tensor"),
        ),
        out_specs=(P("tensor", "dp"), P("dp", "tensor"), P("dp", "tensor")),
        check_vma=False,
    )
```

time: 77.3 us -> 71.2 us (0.921)
  the two profiles are of different devices: /device:TPU:3 before, /device:TPU:0 now
where the time goes in v1:
time: 71.2 us; the launch traced here: 70.4 us
  Pallas kernels  69.8 us (98%)
    pallas_call x1, Pallas kernels, shards(): pl.pallas_call(functools.partial(exchange, n_dp, n_t), out_shape=tuple((p...  65.2 us
    pallas_call x1, Pallas kernels, shards(): pl.pallas_call(finish, out_shape=(jax.ShapeDtypeStruct((hidden, block), b...  4.6 us

profile of v1, /device:TPU:0, one launch (start us, length us, event | category | flops | bytes accessed | tf_op | source)
XLA Modules:
  0.0 70.4 jit_solution(6643760144106320357)
XLA Ops:
  0.6 65.2 %shard_map.94 = (bf16[2048,1024]{1,0:T(8,128)(2,1)S(1)}, bf16[1024,1536]{1,0:T(8,128)(2,1)S(1)}, bf16[1024,1536]{1,0:T(8,128)(2,1)S(1)}, bf16[1024,640]{1,0:T(8,...) custom-call(bf16[160,512]{1,0:T(8,128)(2,1)} %bitcast.7, bf16[160,512]{1,0:T(8,128)(2,1)} %bitcast.8, ...), custom_call_target="tpu_custom_call" | custom-call | flops 9395240960 | bytes 20000000 | tf_op jit(solution)/shard_map/pallas_call | solution.py:588
  65.8 4.6 %shard_map.95 = (bf16[2048,1024]{1,0:T(8,128)(2,1)}, bf16[1024,2048]{1,0:T(8,128)(2,1)}, bf16[1024,2048]{1,0:T(8,128)(2,1)}) custom-call(bf16[2048,1024]{1,0:T(8,128)(2,1)S(1)} %get-tuple-element.9.down_in, bf16[1024,1536]{1,0:T(8,128)(2,1)S(1)} %get-tuple-element.10.gate_in, bf16[1024,1536]{1,0:T(8,128)(2,1)S(1)} %get-tuple-element.11.up_in, ...), custom_call_target="tpu_custom_call" | custom-call | tf_op jit(solution)/shard_map/pallas_call | solution.py:625

commit v2 on v1

--- a/solution.py
+++ b/solution.py
@@ -13,13 +13,14 @@
 EARLY = 4
 HELD = 1
 LATE = 8
+AHEAD = 3
 TAIL = 2
 SPLIT = 2
-LAG = 3
+LAG = 2
 
 
 def exchange(n_dp, n_t, out_hbm, in_hbm, silu_hbm, up_hbm, code_hbm, spread_hbm, w_hbm,
-             down, gate_main, up_main, turned, gate_all, up_all,
+             down, gate_main, up_main, turned, both_all,
              og, li, silu, up, codes, spread, w, slopes_up, acc, hid_all, xin, xout,
              l_sem, w_sem, u_send, u_recv, d_send, d_recv, y_send, y_recv,
              x_send, c_recv, zu_send, zd_send, cy_send, cy_recv, o_sem, o_send, o_recv,
@@ -33,8 +34,9 @@
     part = cols // SPLIT
     total = n_dp * tokens
     n_in, n_out = n_dp * SPLIT, (n_dp - 2) * SPLIT
-    acts = (hid_all, gate_all, up_all)
-    pieces = (EARLY, LATE, LATE)
+    acts = (hid_all, both_all)
+    pieces = (EARLY, LATE)
+    size = hidden // LATE
 
     d = lax.axis_index("dp")
     t = lax.axis_index("tensor")
@@ -89,9 +91,6 @@
         f = span(j, fw)
         return pltpu.make_async_copy(w_hbm.at[f], w.at[f], w_sem.at[j])
 
-    for j in range(hidden // fw):
-        w_copy(j).start()
-
     barrier = pltpu.get_barrier_semaphore()
     greet = [(d, y_peer), (partner, t)]
     greet += [(chip_at(r), t) for r in range(1, chips)]
@@ -192,7 +191,7 @@
                       x_send.at[SPLIT + h], c_recv.at[out_slot + h], far_owner, t)
 
     def f_part(a, j):
-        return span(j, hidden // pieces[a])
+        return span(j, acts[a].shape[2] // pieces[a])
 
     def own_chip(a, j, r):
         own = acts[a].at[d, :, f_part(a, j)]
@@ -238,6 +237,8 @@
 
     lax.fori_loop(0, EARLY, early, 0)
 
+    for j in range(hidden // fw):
+        w_copy(j).start()
     loads[4].wait()
     loads[5].wait()
     acc[...] = jnp.zeros_like(acc)
@@ -295,20 +296,45 @@
 
         side.start()
 
+    def head_rows(i, carry):
+        up_next, down_next, side = chain(i, 0, in_ref)
+        go_up, go_down = goes(in_head)
+        up_next.wait_recv()
+
+        @pl.when(go_up)
+        def _():
+            up_next.start()
+
+        @pl.when(go_down)
+        def _():
+            down_next.start()
+        return carry
+
+    def head_side(i, carry):
+        chain(i, 0, in_ref)[2].start()
+        return carry
+
     in_far = lax.max(z - in_head, in_head - z)
     out_far = lax.max(z - out_head, out_head - z)
     at_in_head = jnp.logical_and(in_chain, in_far == 0)
 
     def matmul_piece(piece):
         k = span(piece, cols)
-
-        def f_step(j, carry):
-            f = span(j, fw)
-            acc[:, f] += lax.dot_general(og[:, k], w[f, k], (((1,), (1,)), ((), ())),
-                                         preferred_element_type=jnp.float32)
-            return carry
-
-        lax.fori_loop(0, hidden // fw, f_step, 0)
+        acc[...] += lax.dot_general(og[:, k], w[:, k], (((1,), (1,)), ((), ())),
+                                    preferred_element_type=jnp.float32)
+
+    def wave_step(s):
+        i = s - 2 * (in_far - 1)
+
+        @pl.when(jnp.logical_and(jnp.logical_and(in_chain, in_far > 0), jnp.logical_and(i >= 0, i < n_in)))
+        def _():
+            chain_step(i, 0, in_ref, in_head)
+
+        o = s - LAG - 2 * out_far
+
+        @pl.when(jnp.logical_and(in_chain, jnp.logical_and(o >= 0, o < n_out)))
+        def _():
+            chain_step(o, n_in, out_ref, out_head)
 
     def gather(s, carry):
         below, above = z >= s, z + s < rows
@@ -343,6 +369,10 @@
             for j in range(EARLY - HELD, EARLY):
                 send_own(0, j)
 
+            @pl.when(at_in_head)
+            def _():
+                lax.fori_loop(0, n_in, head_rows, 0)
+
         @pl.when(s == 1)
         def _():
             for j in range(hidden // fw):
@@ -350,18 +380,18 @@
 
         @pl.when(jnp.logical_and(s == rows - 1, at_in_head))
         def _():
-            def start(i, carry):
-                chain_step(i, 0, in_ref, in_head)
-                return carry
-
-            lax.fori_loop(0, n_in, start, 0)
+            lax.fori_loop(0, n_in, head_side, 0)
+
+        @pl.when(s >= rows)
+        def _():
+            wave_step(s - rows)
 
         def piece_step(k, carry):
             side = k >= 3
-            dist = jnp.where(k == 0, 0, jnp.where(side, s - 1, s))
+            dist = jnp.where(k == 0, 0, jnp.where(side, s - 2, s))
             down_side = jnp.logical_or(k == 1, k == 3)
             row = jnp.where(down_side, z - dist, z + dist)
-            wanted = jnp.where(k == 0, s == 1, jnp.logical_or(dist > 0, down_side))
+            wanted = jnp.where(k == 0, s == 1, jnp.logical_or(dist > 0, jnp.logical_and(dist == 0, down_side)))
             valid = jnp.logical_and(wanted, jnp.logical_and(row >= 0, row < rows))
 
             @pl.when(valid)
@@ -377,48 +407,42 @@
         lax.fori_loop(0, 5, piece_step, 0)
         return carry
 
-    lax.fori_loop(1, rows + 1, gather, 0)
+    lax.fori_loop(1, rows + 2, gather, 0)
 
     o_own = pltpu.make_async_copy(og.at[:, span(d, block)], xout.at[d], o_sem)
     o_own.start()
     o_other = remote(og.at[:, span(partner, block)], xout.at[d], o_send, o_recv, partner, t)
     o_other.start()
 
-    def late(j):
-        f = f_part(1, j)
+    def late(j, carry):
+        f = span(j, size)
         grad = acc[:, f]
-        gate_all[d, :, f] = (grad * slopes_up[:, f]).astype(jnp.bfloat16)
-        up_all[d, :, f] = (grad * silu[:, f].astype(jnp.float32)).astype(jnp.bfloat16)
+        both_all[d, :, span(2 * j, size)] = (grad * slopes_up[:, f]).astype(jnp.bfloat16)
+        both_all[d, :, span(2 * j + 1, size)] = (grad * silu[:, f].astype(jnp.float32)).astype(jnp.bfloat16)
         send_own(1, j)
-        send_own(2, j)
-
-    steps = max(n_in + rows - 2, n_out + LAG + rows - 1, LATE)
+        return carry
+
+    lax.fori_loop(0, LATE, late, 0)
+
+    steps = max(n_in + 2 * (rows - 2), n_out + LAG + 2 * (rows - 1))
 
     def wave(s, carry):
-        @pl.when(s < LATE)
-        def _():
-            late(s)
-
-        i = s - (in_far - 1)
-
-        @pl.when(jnp.logical_and(jnp.logical_and(in_chain, in_far > 0), jnp.logical_and(i >= 0, i < n_in)))
-        def _():
-            chain_step(i, 0, in_ref, in_head)
-
-        o = s - LAG - out_far
-
-        @pl.when(jnp.logical_and(in_chain, jnp.logical_and(o >= 0, o < n_out)))
-        def _():
-            chain_step(o, n_in, out_ref, out_head)
-        return carry
-
-    lax.fori_loop(0, steps, wave, 0)
+        wave_step(s)
+        return carry
+
+    lax.fori_loop(2, steps, wave, 0)
 
     def hidden_relay(j, carry):
         relay(0, j)
         return carry
 
     lax.fori_loop(0, EARLY, hidden_relay, 0)
+
+    def late_relay(j, carry):
+        relay(1, j)
+        return carry
+
+    lax.fori_loop(0, AHEAD, late_relay, 0)
 
     def side_wait(i, base, ref):
         @pl.when(has_side)
@@ -460,23 +484,22 @@
     turned[...] = xin[...].reshape(total, block).T
 
     def main_step(j, carry):
-        relay(1, j)
-        relay(2, j)
+        @pl.when(j >= AHEAD)
+        def _():
+            relay(1, j)
 
         @pl.when(j > 0)
         def _():
-            for a in (1, 2):
-                from_partner(a)(j - 1, 0)
-            f = f_part(1, j - 1)
-            size = hidden // LATE
-            gate_main[:, f] = product(turned[...], gate_all[:, :, f].reshape(total, size))
-            up_main[:, f] = product(turned[...], up_all[:, :, f].reshape(total, size))
+            from_partner(1)(j - 1, 0)
+            f = span(j - 1, size)
+            result = product(turned[...], both_all[:, :, f_part(1, j - 1)].reshape(total, 2 * size))
+            gate_main[:, f] = result[:, :size]
+            up_main[:, f] = result[:, size:]
         return carry
 
     lax.fori_loop(0, LATE - TAIL + 1, main_step, 0)
     for j in range(LATE - TAIL + 1, LATE):
         relay(1, j)
-        relay(2, j)
 
     def gather_end(s, carry):
         for h in range(SPLIT):
@@ -539,17 +562,16 @@
             return carry
         return step
 
-    for a in range(3):
+    for a in range(2):
         lax.fori_loop(0, pieces[a], sent(a), 0)
-    for a in (1, 2):
-        lax.fori_loop(LATE - TAIL, LATE, from_partner(a), 0)
-
-
-def finish(down_in, gate_in, up_in, turned, gate_all, up_all, down_out, gate_out, up_out, gate_tail, up_tail, sems):
-    n_dp, tokens, hidden = gate_all.shape
+    lax.fori_loop(LATE - TAIL, LATE, from_partner(1), 0)
+
+
+def finish(down_in, gate_in, up_in, turned, both_all, down_out, gate_out, up_out, gate_tail, up_tail, sems):
+    n_dp, tokens, hidden2 = both_all.shape
     total = n_dp * tokens
     main = gate_in.shape[1]
-    size = (hidden - main) // TAIL
+    size = hidden2 // 2 // LATE
     copies = [
         pltpu.make_async_copy(down_in, down_out, sems.at[0]),
         pltpu.make_async_copy(gate_in, gate_out.at[:, :main], sems.at[1]),
@@ -559,9 +581,11 @@
         copy.start()
     for j in range(TAIL):
         f = slice(main + j * size, main + (j + 1) * size)
-        for k, (acts, tail, out) in enumerate(((gate_all, gate_tail, gate_out), (up_all, up_tail, up_out))):
-            tail[j] = jnp.dot(turned[...], acts[:, :, f].reshape(total, size),
-                              preferred_element_type=jnp.float32).astype(jnp.bfloat16)
+        acts = both_all[:, :, 2 * f.start:2 * f.stop].reshape(total, 2 * size)
+        result = jnp.dot(turned[...], acts, preferred_element_type=jnp.float32).astype(jnp.bfloat16)
+        gate_tail[j] = result[:, :size]
+        up_tail[j] = result[:, size:]
+        for k, (tail, out) in enumerate(((gate_tail, gate_out), (up_tail, up_out))):
             copies.append(pltpu.make_async_copy(tail.at[j], out.at[:, f], sems.at[3 + j * 2 + k]))
             copies[-1].start()
     for copy in copies:
@@ -589,9 +613,9 @@
         functools.partial(exchange, n_dp, n_t),
         out_shape=tuple(pltpu.VMEM(shape, bf16) for shape in (
             (hidden, block), (block, main), (block, main), (block, total),
-            (n_dp, tokens, hidden), (n_dp, tokens, hidden))),
+            (n_dp, tokens, 2 * hidden))),
         in_specs=[anywhere] * 7,
-        out_specs=[vmem] * 6,
+        out_specs=[vmem] * 5,
         scratch_shapes=[
             pltpu.VMEM((tokens, width), bf16),
             pltpu.VMEM((tokens, cols), bf16),
@@ -610,7 +634,7 @@
             dma((rows, SPLIT)), dma((rows, SPLIT)),
             dma((2 * SPLIT,)), dma((units,)), dma((units,)), dma((units,)), dma((units,)), dma((units,)),
             dma, dma, dma,
-            dma((3, far, LATE)), dma((3, far, LATE)), dma((3, chips, LATE)), dma((3, chips, LATE)),
+            dma((2, far, LATE)), dma((2, far, LATE)), dma((2, chips, LATE)), dma((2, chips, LATE)),
         ],
         compiler_params=pltpu.CompilerParams(
             collective_id=0, has_side_effects=True, vmem_limit_bytes=38 * 1024 * 1024),
@@ -625,7 +649,7 @@
     return pl.pallas_call(
         finish,
         out_shape=(jax.ShapeDtypeStruct((hidden, block), bf16), across, across),
-        in_specs=[vmem] * 6,
+        in_specs=[vmem] * 5,
         out_specs=[anywhere] * 3,
         scratch_shapes=[
             pltpu.VMEM((TAIL, block, size), bf16), pltpu.VMEM((TAIL, block, size), bf16), dma((3 + 2 * TAIL,))],

time: 71.2 us -> 62.9 us (0.88)
  Pallas kernels: 69.8 us -> 62.1 us
    pallas_call x1, Pallas kernels: 65.2 us -> 57.5 us  [shards(): pl.pallas_call(functools.partial(exchange, n_dp, n_t), out_shape=tuple((p...]
where the time goes in v2:
time: 62.9 us; the launch traced here: 62.8 us
  Pallas kernels  62.1 us (99%)
  between operations  0.64 us (1%)
    pallas_call x1, Pallas kernels, shards(): pl.pallas_call(functools.partial(exchange, n_dp, n_t), out_shape=tuple((p...  57.5 us
    pallas_call x1, Pallas kernels, shards(): pl.pallas_call(finish, out_shape=(jax.ShapeDtypeStruct((hidden, block), b...  4.6 us

profile of v2, /device:TPU:0, one launch (start us, length us, event | category | flops | bytes accessed | tf_op | source)
XLA Modules:
  0.0 62.8 jit_solution(13408168030528701885)
XLA Ops:
  0.6 57.5 %shard_map.94 = (bf16[2048,1024]{1,0:T(8,128)(2,1)S(1)}, bf16[1024,1536]{1,0:T(8,128)(2,1)S(1)}, bf16[1024,1536]{1,0:T(8,128)(2,1)S(1)}, bf16[1024,640]{1,0:T(8,128)(2,1)S(1)}, bf16[4,160,4096]{2,1,0:T(8,128)(2,1)S(1)}) custom-call(bf16[160,512]{1,0:T(8,128)(2,1)} %bitcast.7, bf16[160,512]{1,0:T(8,128)(2,1)} %bitcast.8, bf16[160,2048]{1,0:T(8,128)(2,1)} %bitcast.5, ...), custom_call_target="tpu_custom_call" | custom-call | flops 9395240960 | bytes 20000000 | tf_op jit(solution)/shard_map/pallas_call | solution.py:612
  58.2 4.6 %shard_map.95 = (bf16[2048,1024]{1,0:T(8,128)(2,1)}, bf16[1024,2048]{1,0:T(8,128)(2,1)}, bf16[1024,2048]{1,0:T(8,128)(2,1)}) custom-call(bf16[2048,1024]{1,0:T(8,128)(2,1)S(1)} %get-tuple-element.8.down_in, bf16[1024,1536]{1,0:T(8,128)(2,1)S(1)} %get-tuple-element.9.gate_in, bf16[1024,1536]{1,0:T(8,128)(2,1)S(1)} %get-tuple-element.10.up_in, ...), custom_call_target="tpu_custom_call" | custom-call | tf_op jit(solution)/shard_map/pallas_call | solution.py:649

commit v3 on v2

v3 whole, which is shorter than its diff:
```python
import functools

import jax
import jax.numpy as jnp
import numpy as np
from jax import lax
from jax.experimental import pallas as pl
from jax.experimental.pallas import tpu as pltpu
from jax.sharding import PartitionSpec as P

SLOPE_LEVELS = (-0.09, 0.06, 0.22, 0.41, 0.6, 0.79, 0.96, 1.08)
MESH = pl.DeviceIdType.MESH
EARLY = 4
HELD = 1
LATE = 8
DOWN_AT = 4
RELAY_AT = 9
THEN = 3
AHEAD = 1
TAIL = 1
OG_SPLIT = 4
SPLIT = 2
IN_PACE = 1
IN_HOP = 3
SIDE_LAG = 2
OUT_PACE = 2
OUT_HOP = 2
WAVE_AT = 0
LAG = 5


def exchange(n_dp, n_t, out_hbm, in_hbm, silu_hbm, up_hbm, code_hbm, spread_hbm, w_hbm,
             down, gate_main, up_main, turned, both_all,
             og, li, silu, up, codes, spread, w, slopes_up, acc, hid_all, xin, xout,
             l_sem, w_sem, u_send, u_recv, d_send, d_recv, y_send, y_recv,
             x_send, c_recv, zu_send, zd_send, cy_send, cy_recv, o_sem, o_send, o_recv,
             ax_send, ac_send, hx_recv, hc_recv, hp_recv, ax_recv, ac_recv, ap_recv):
    chips = n_dp // 2
    rows = n_t // 2
    ratio = n_t // n_dp
    tokens, cols = out_hbm.shape
    hidden, width = w_hbm.shape
    block = width // n_dp
    part = cols // SPLIT
    fine = min(OG_SPLIT, cols // 128)
    total = n_dp * tokens
    n_in, n_out = n_dp * SPLIT, (n_dp - 2) * SPLIT
    n_all = n_out * ratio
    acts = (hid_all, both_all)
    pieces = (EARLY, LATE)
    size = hidden // LATE

    d = lax.axis_index("dp")
    t = lax.axis_index("tensor")
    q, c = d // 2, lax.rem(d, 2)
    z, y = t // 2, lax.rem(t, 2)
    partner = q * 2 + (1 - c)
    y_peer = z * 2 + (1 - y)
    z_up = lax.min(z + 1, rows - 1) * 2 + y
    z_down = lax.max(z - 1, 0) * 2 + y
    has_up, has_down = z + 1 < rows, z > 0
    owner = t // ratio
    if ratio == 2:
        in_chain = d >= 0
        has_side = d >= 0
        chain_col, side_col = y, 1 - y
    else:
        in_chain = lax.rem(d, 2) == y
        has_side = lax.rem(d, 2) != y
        chain_col, side_col = y * 0, y * 0
    in_head = (d * ratio) // 2
    out_head = lax.rem(in_head + rows // 2, rows)

    def chip_at(r):
        return lax.rem(q + r, chips) * 2 + c

    def group_from(r, core):
        return lax.rem(q + chips - r, chips) * 2 + core

    def span(index, size):
        return pl.ds(pl.multiple_of(index * size, 128), size)

    def remote(src, dst, send, recv, dp, tensor):
        return pltpu.make_async_remote_copy(
            src_ref=src, dst_ref=dst, send_sem=send, recv_sem=recv,
            device_id={"dp": dp, "tensor": tensor}, device_id_type=MESH)

    my_cols = og.at[:, span(t, cols)]
    loads = [
        pltpu.make_async_copy(out_hbm, my_cols, l_sem.at[0]),
        pltpu.make_async_copy(in_hbm, li, l_sem.at[1]),
        pltpu.make_async_copy(silu_hbm, silu, l_sem.at[2]),
        pltpu.make_async_copy(up_hbm, up, l_sem.at[3]),
        pltpu.make_async_copy(code_hbm, codes, l_sem.at[4]),
        pltpu.make_async_copy(spread_hbm, spread, l_sem.at[5]),
    ]
    for load in loads:
        load.start()

    fw = min(512, hidden)

    def w_copy(j):
        f = span(j, fw)
        return pltpu.make_async_copy(w_hbm.at[f], w.at[f], w_sem)

    barrier = pltpu.get_barrier_semaphore()
    greet = [(d, y_peer), (partner, t)]
    greet += [(chip_at(r), t) for r in range(1, chips)]
    for r in range(1, chips):
        greet.append((lax.rem(q + r, chips) * 2 + 1 - c, t))
    for dp, tensor in greet:
        pl.semaphore_signal(barrier, inc=1, device_id={"dp": dp, "tensor": tensor}, device_id_type=MESH)

    @pl.when(has_up)
    def _():
        pl.semaphore_signal(barrier, inc=1, device_id={"dp": d, "tensor": z_up}, device_id_type=MESH)

    @pl.when(has_down)
    def _():
        pl.semaphore_signal(barrier, inc=1, device_id={"dp": d, "tensor": z_down}, device_id_type=MESH)

    at_end = jnp.logical_or(z == 0, z == rows - 1)

    pl.semaphore_wait(barrier, len(greet) + has_up.astype(jnp.int32) + has_down.astype(jnp.int32))

    def og_piece(row, col, h):
        return og.at[:, span((row * 2 + col) * fine + h, cols // fine)]

    def up_copy(s, h):
        piece = og_piece(lax.max(z - s + 1, 0), y, h)
        return remote(piece, piece, u_send, u_recv.at[s - 1, h], d, z_up)

    def down_copy(s, h):
        piece = og_piece(lax.min(z + s - 1, rows - 1), y, h)
        return remote(piece, piece, d_send, d_recv.at[s - 1, h], d, z_down)

    def up_wait(s, h):
        piece = og_piece(lax.max(z - s, 0), y, h)
        return remote(piece, piece, u_send, u_recv.at[s - 1, h], d, z_up)

    def down_wait(s, h):
        piece = og_piece(lax.min(z + s, rows - 1), y, h)
        return remote(piece, piece, d_send, d_recv.at[s - 1, h], d, z_down)

    def across(row, h):
        piece = og_piece(row, y, h)
        return remote(piece, piece, y_send, y_recv.at[row], d, y_peer)

    def across_wait(row):
        piece = og.at[:, span(row * 2 + 1 - y, cols)]
        return remote(piece, piece, y_send, y_recv.at[row], d, y_peer)

    loads[0].wait()

    for h in range(fine):
        across(z, h).start()

        @pl.when(has_up)
        def _():
            up_copy(1, h).start()

        @pl.when(has_down)
        def _():
            down_copy(1, h).start()

    def in_piece(group, col, h):
        return xin.at[group, :, span(col * SPLIT + h, part)]

    def out_piece(group, col, h):
        return xout.at[group, :, span(col * SPLIT + h, part)]

    in_slot = (lax.rem(owner // 2 + chips - q, chips) * 2 + c) * SPLIT

    def li_remote(h):
        return remote(li.at[:, h * part:(h + 1) * part], in_piece(d, chain_col_of(t), h),
                      x_send.at[0], c_recv.at[in_slot + h], owner, t)

    def li_local(h):
        return pltpu.make_async_copy(li.at[:, h * part:(h + 1) * part], in_piece(d, chain_col_of(t), h),
                                     c_recv.at[in_slot + h])

    def chain_col_of(tensor):
        return lax.rem(tensor, 2) if ratio == 2 else tensor * 0

    loads[1].wait()
    owned = owner == d

    @pl.when(owned)
    def _():
        for h in range(SPLIT):
            li_local(h).start()

    @pl.when(jnp.logical_not(owned))
    def _():
        for h in range(SPLIT):
            li_remote(h).start()

    far_row = lax.rem(z + rows // 2, rows)
    far_owner = (far_row * 2 + y) // ratio
    crosses = far_owner // 2 != q
    far_dist = lax.max(lax.rem(far_owner // 2 + chips - q, chips), 1)
    out_slot = n_in + ((far_dist - 1) * 2 + c) * SPLIT

    def og_far(h):
        src = og.at[:, span((far_row * 2 + y) * SPLIT + h, part)]
        return remote(src, out_piece(d, chain_col_of(t), h),
                      x_send.at[1], c_recv.at[out_slot + h], far_owner, t)

    def f_part(a, j):
        return span(j, acts[a].shape[2] // pieces[a])

    def own_chip(a, j, r):
        own = acts[a].at[d, :, f_part(a, j)]
        land = hx_recv.at[r - 1] if a == 0 else ax_recv.at[r - 1, j]
        return remote(own, own, ax_send.at[a, r - 1], land, chip_at(r), t)

    def own_core(a, j):
        own = acts[a].at[d, :, f_part(a, j)]
        return remote(own, own, ac_send.at[a, 0], (ac_recv if a else hc_recv), partner, t)

    def send_own(a, j):
        for r in range(1, chips):
            own_chip(a, j, r).start()
        own_core(a, j).start()

    def chip_hidden(r):
        land = hid_all.at[group_from(r, c)]
        return remote(land, land, ac_send.at[0, r], hx_recv.at[r - 1], partner, t)

    def pass_hidden(r, core):
        land = hid_all.at[group_from(r, core)]
        return remote(land, land, ac_send.at[0, r], hp_recv.at[r - 1], partner, t)

    def chip_late(j, r):
        land = both_all.at[group_from(r, c), :, f_part(1, j)]
        return remote(land, land, ac_send.at[1, r], ax_recv.at[r - 1, j], partner, t)

    def pass_late(j, r, core):
        land = both_all.at[group_from(r, core), :, f_part(1, j)]
        return remote(land, land, ac_send.at[1, r], ap_recv.at[r - 1, j], partner, t)

    def relay(j):
        for r in range(1, chips):
            chip_late(j, r).wait_recv()
            pass_late(j, r, c).start()

    def arrived(j):
        for r in range(1, chips):
            pass_late(j, r, 1 - c).wait_recv()

    loads[2].wait()
    loads[3].wait()
    for j in range(hidden // fw):
        w_copy(j).start()

    def early(j, carry):
        f = f_part(0, j)
        hid_all[d, :, f] = (silu[:, f].astype(jnp.float32) * up[:, f].astype(jnp.float32)).astype(jnp.bfloat16)

        @pl.when(j < EARLY - HELD)
        def _():
            send_own(0, j)
        return carry

    lax.fori_loop(0, EARLY, early, 0)

    loads[4].wait()
    loads[5].wait()
    acc[...] = jnp.zeros_like(acc)

    def decode(j, carry):
        f = span(j, fw)
        words = codes[:, f]
        symbols = jnp.dot(
            spread[...],
            jnp.concatenate([((words >> (3 * k)) & 7).astype(jnp.float32).astype(jnp.bfloat16) for k in range(10)], axis=0),
            preferred_element_type=jnp.float32)
        slopes = jnp.full(symbols.shape, SLOPE_LEVELS[0], jnp.float32)
        for s in range(1, 8):
            slopes = jnp.where(symbols > s - 0.5, jnp.float32(SLOPE_LEVELS[s]), slopes)
        slopes_up[:, f] = up[:, f].astype(jnp.float32) * slopes
        return carry

    lax.fori_loop(0, hidden // fw, decode, 0)

    def unit(i):
        h, u = lax.rem(i, SPLIT), i // SPLIT
        return lax.rem(u, 2), u // 2, h

    def in_ref(i, col):
        core, r, h = unit(i)
        return in_piece(group_from(r, core), col, h)

    def in_copies(i):
        piece = in_ref(i, chain_col)
        return (remote(piece, piece, zu_send.at[0], c_recv.at[i], d, z_up),
                remote(piece, piece, zd_send.at[0], c_recv.at[i], d, z_down),
                remote(piece, piece, cy_send.at[0], cy_recv, d, y_peer))

    in_up = jnp.logical_and(in_chain, jnp.logical_and(z >= in_head, has_up))
    in_down = jnp.logical_and(in_chain, jnp.logical_and(z <= in_head, has_down))

    def in_rows(i):
        up_next, down_next, side = in_copies(i)
        up_next.wait_recv()

        @pl.when(in_up)
        def _():
            up_next.start()

        @pl.when(in_down)
        def _():
            down_next.start()

    def head_wait(i, carry):
        in_copies(i)[0].wait_recv()
        return carry

    def head_up(i, carry):
        in_copies(i)[0].start()
        return carry

    def head_down(i, carry):
        in_copies(i)[1].start()
        return carry

    def in_side(i, carry):
        in_copies(i)[2].start()
        return carry

    out_up = jnp.logical_and(z >= out_head, has_up)
    out_down = jnp.logical_and(z <= out_head, has_down)
    at_out_head = z == out_head

    in_far = lax.max(z - in_head, in_head - z)
    out_far = lax.max(z - out_head, out_head - z)
    out_last = jnp.logical_and(at_end, out_far > jnp.where(in_chain, in_far, 0))

    def out_step(i):
        if ratio == 2:
            native, other = i < n_out, i + n_out
            col = jnp.where(native, y, 1 - y)
        else:
            native, other, col = in_chain, i, y * 0
        core, r, h = unit(lax.rem(i, n_out))
        piece = out_piece(group_from(r + 1, core), col, h)
        n = n_in + i
        up_next = remote(piece, piece, zu_send.at[1], c_recv.at[n], d, z_up)
        down_next = remote(piece, piece, zd_send.at[1], c_recv.at[n], d, z_down)
        side = remote(piece, piece, cy_send.at[1], c_recv.at[n_in + lax.min(other, n_all - 1)], d, y_peer)
        up_next.wait_recv()

        @pl.when(jnp.logical_and(native, at_out_head))
        def _():
            side.start()

        @pl.when(out_up)
        def _():
            up_next.start()

        @pl.when(out_down)
        def _():
            down_next.start()

    at_in_head = jnp.logical_and(in_chain, in_far == 0)

    def matmul_piece(piece):
        k = span(piece, cols)
        acc[...] += lax.dot_general(og[:, k], w[:, k], (((1,), (1,)), ((), ())),
                                    preferred_element_type=jnp.float32)

    def wave_step(s):
        past = jnp.logical_and(in_chain, in_far > 0)
        first = IN_PACE * (s - IN_HOP * (in_far - 1))
        for i in range(IN_PACE):
            @pl.when(jnp.logical_and(past, jnp.logical_and(first + i >= 0, first + i < n_in)))
            def _():
                in_rows(first + i)

        late_side = first - IN_PACE * SIDE_LAG
        for i in range(IN_PACE):
            @pl.when(jnp.logical_and(past, jnp.logical_and(late_side + i >= 0, late_side + i < n_in)))
            def _():
                in_side(late_side + i, 0)

        out_first = OUT_PACE * (s - LAG - OUT_HOP * out_far)
        for i in range(OUT_PACE):
            @pl.when(jnp.logical_and(jnp.logical_not(out_last), jnp.logical_and(out_first + i >= 0, out_first + i < n_all)))
            def _():
                out_step(out_first + i)

    order, place = [], 0
    for dist in range(rows + 1):
        for far_side in (0, 1):
            away = dist - far_side
            for way in ((-1, 1) if away > 0 else (1,) if away == 0 else ()):
                row = z + way * away
                valid = jnp.logical_and(row >= 0, row < rows)
                order.append((valid, place, row, far_side))
                place = place + valid.astype(jnp.int32)

    def multiply(p):
        row, side = 0, 0
        for valid, place, its_row, far_side in order:
            mine = jnp.logical_and(valid, place == p)
            row = jnp.where(mine, its_row, row)
            side = jnp.where(mine, far_side, side)

        @pl.when(side == 1)
        def _():
            across_wait(row).wait_recv()

        matmul_piece(row * 2 + jnp.where(side == 1, 1 - y, y))

    arrivals = fine * (rows - 1)

    def gather(e, carry):
        s, h = e // fine + 1, lax.rem(e, fine)
        last_part = h == fine - 1

        @pl.when(z >= s)
        def _():
            up_wait(s, h).wait_recv()

            @pl.when(has_up)
            def _():
                up_copy(s + 1, h).start()

            across(lax.max(z - s, 0), h).start()

        @pl.when(z + s < rows)
        def _():
            down_wait(s, h).wait_recv()

            @pl.when(has_down)
            def _():
                down_copy(s + 1, h).start()

            across(lax.min(z + s, rows - 1), h).start()

        @pl.when(jnp.logical_and(s == rows // 2, last_part))
        def _():
            @pl.when(crosses)
            def _():
                for k in range(SPLIT):
                    og_far(k).start()

            for j in range(EARLY - HELD, EARLY):
                send_own(0, j)

        @pl.when(jnp.logical_and(last_part, at_in_head))
        def _():
            @pl.when(s == 1)
            def _():
                lax.fori_loop(near, n_in, head_wait, 0)

            @pl.when(jnp.logical_and(in_up, s == lax.max(z, 1)))
            def _():
                lax.fori_loop(jnp.where(z == 0, near, 0), n_in, head_up, 0)

            @pl.when(jnp.logical_and(in_down, s == lax.max(rows - 1 - z, 1)))
            def _():
                lax.fori_loop(jnp.where(z == rows - 1, near, 0), n_in, head_down, 0)

        @pl.when(jnp.logical_and(jnp.logical_and(s == rows - 1, last_part), at_in_head))
        def _():
            lax.fori_loop(0, n_in, in_side, 0)

        @pl.when(e == fine - 1)
        def _():
            pltpu.make_async_copy(w_hbm, w, w_sem).wait()

        pace = max(fine // 2, 1)
        p = jnp.where(e < arrivals, (e + 1) // pace - 2, e - arrivals + arrivals // pace - 1)
        now = jnp.logical_and(p >= 0, jnp.logical_or(e >= arrivals, lax.rem(e + 1, pace) == 0))

        @pl.when(jnp.logical_and(now, p >= 3 + WAVE_AT))
        def _():
            wave_step(p - 3 - WAVE_AT)

        @pl.when(now)
        def _():
            multiply(p)
        return carry

    near = 2 * SPLIT

    @pl.when(at_in_head)
    def _():
        lax.fori_loop(0, near, head_wait, 0)

        @pl.when(z == 0)
        def _():
            lax.fori_loop(0, near, head_up, 0)

        @pl.when(z == rows - 1)
        def _():
            lax.fori_loop(0, near, head_down, 0)

    lax.fori_loop(0, arrivals + n_t - arrivals // max(fine // 2, 1) + 1, gather, 0)

    o_own = pltpu.make_async_copy(og.at[:, span(d, block)], xout.at[d], o_sem)
    o_own.start()
    o_other = remote(og.at[:, span(partner, block)], xout.at[d], o_send, o_recv, partner, t)
    o_other.start()

    def late(j, carry):
        f = span(j, size)
        grad = acc[:, f]
        both_all[d, :, span(2 * j, size)] = (grad * slopes_up[:, f]).astype(jnp.bfloat16)
        both_all[d, :, span(2 * j + 1, size)] = (grad * silu[:, f].astype(jnp.float32)).astype(jnp.bfloat16)
        send_own(1, j)
        return carry

    lax.fori_loop(0, LATE, late, 0)

    steps = max(-(-n_in // IN_PACE) + SIDE_LAG + IN_HOP * (rows - 2), -(-n_all // OUT_PACE) + LAG + OUT_HOP * (rows - 1))

    def wave(s, carry):
        @pl.when(s == RELAY_AT)
        def _():
            for r in range(1, chips):
                chip_hidden(r).wait_recv()
                pass_hidden(r, c).start()

        wave_step(s)
        return carry

    lax.fori_loop(n_t - 3 - WAVE_AT, steps, wave, 0)

    def late_relay(j, carry):
        relay(j)
        return carry

    lax.fori_loop(0, AHEAD, late_relay, 0)

    def product(left, right):
        return jnp.dot(left, right, preferred_element_type=jnp.float32).astype(jnp.bfloat16)

    def down_product():
        o_own.wait()
        o_other.wait()
        theirs = hid_all.at[partner]
        remote(theirs, theirs, ac_send.at[0, 0], hc_recv, partner, t).wait_recv()
        for r in range(1, chips):
            pass_hidden(r, 1 - c).wait_recv()

        def down_step(j, carry):
            f = span(j, fw)
            down[f, :] = product(hid_all[:, :, f].reshape(total, fw).T, xout[...].reshape(total, block))
            return carry

        lax.fori_loop(0, hidden // fw, down_step, 0)

    @pl.when(jnp.logical_not(out_last))
    def _():
        down_product()

    lax.fori_loop(AHEAD, THEN, late_relay, 0)
    columns = xin.at[:, :, :cols]

    @pl.when(has_side)
    def _():
        remote(columns, columns, cy_send.at[0], cy_recv, d, y_peer).wait_recv()

    turned[...] = xin[...].reshape(total, block).T
    theirs_late = both_all.at[partner]
    remote(theirs_late, theirs_late, ac_send.at[1, 0], ac_recv, partner, t).wait_recv()

    def main_step(j, carry):
        @pl.when(j >= THEN)
        def _():
            relay(j)

        @pl.when(j > 0)
        def _():
            arrived(j - 1)
            f = span(j - 1, size)
            result = product(turned[...], both_all[:, :, f_part(1, j - 1)].reshape(total, 2 * size))
            gate_main[:, f] = result[:, :size]
            up_main[:, f] = result[:, size:]
        return carry

    lax.fori_loop(0, DOWN_AT, main_step, 0)

    @pl.when(out_last)
    def _():
        def take(i, carry):
            out_step(i)
            return carry

        lax.fori_loop(0, n_all, take, 0)
        down_product()

    lax.fori_loop(DOWN_AT, LATE - TAIL + 1, main_step, 0)

    def sent(ref, sem):
        remote(ref, ref, sem, c_recv.at[0], partner, t).wait_send()

    for k in range(rows):
        ups = k + 1
        downs = rows - k

        @pl.when(jnp.logical_and(z == k, has_up))
        def _():
            sent(og.at[:, :ups * cols], u_send)

        @pl.when(jnp.logical_and(z == k, has_down))
        def _():
            sent(og.at[:, :downs * cols], d_send)

    sent(og.at[:, :rows * cols], y_send)

    @pl.when(jnp.logical_not(owned))
    def _():
        sent(li, x_send.at[0])

    @pl.when(crosses)
    def _():
        sent(li, x_send.at[1])

    far_out = xout.at[:n_dp - 2]
    for flag, ref, sem in (
            (in_up, columns, zu_send.at[0]), (in_down, columns, zd_send.at[0]), (in_chain, columns, cy_send.at[0]),
            (out_up, far_out, zu_send.at[1]), (out_down, far_out, zd_send.at[1]),
            (jnp.logical_and(in_chain, at_out_head), xout.at[:n_dp - 2, :, :cols], cy_send.at[1])):
        @pl.when(flag)
        def _():
            sent(ref, sem)

    for a in range(2):
        own = acts[a].at[d]
        sent(own, ac_send.at[a, 0])
        for r in range(1, chips):
            sent(own, ax_send.at[a, r - 1])
            if a == 0:
                sent(own, ac_send.at[0, r])
    for j in range(LATE - TAIL + 1, LATE):
        relay(j)
    for j in range(LATE - TAIL, LATE):
        arrived(j)
    for r in range(1, chips):
        sent(both_all.at[d], ac_send.at[1, r])


def finish(down_in, gate_in, up_in, turned, both_all, down_out, gate_out, up_out, gate_tail, up_tail, sems):
    n_dp, tokens, hidden2 = both_all.shape
    total = n_dp * tokens
    main = gate_in.shape[1]
    size = hidden2 // 2 // LATE
    copies = [
        pltpu.make_async_copy(down_in, down_out, sems.at[0]),
        pltpu.make_async_copy(gate_in, gate_out.at[:, :main], sems.at[1]),
        pltpu.make_async_copy(up_in, up_out.at[:, :main], sems.at[2]),
    ]
    for copy in copies:
        copy.start()
    for j in range(TAIL):
        f = slice(main + j * size, main + (j + 1) * size)
        acts = both_all[:, :, 2 * f.start:2 * f.stop].reshape(total, 2 * size)
        result = jnp.dot(turned[...], acts, preferred_element_type=jnp.float32).astype(jnp.bfloat16)
        gate_tail[j] = result[:, :size]
        up_tail[j] = result[:, size:]
        for k, (tail, out) in enumerate(((gate_tail, gate_out), (up_tail, up_out))):
            copies.append(pltpu.make_async_copy(tail.at[j], out.at[:, f], sems.at[3 + j * 2 + k]))
            copies[-1].start()
    for copy in copies:
        copy.wait()


def shards(n_dp, n_t, out_grad, layer_input, w_down, silu_gate, up_proj, slope_codes):
    hidden, width = w_down.shape
    cols = out_grad.shape[2]
    tokens = out_grad.shape[0] * out_grad.shape[1]
    chips, rows, block = n_dp // 2, n_t // 2, width // n_dp
    words = tokens // 10
    total = n_dp * tokens
    row, col = np.arange(tokens)[:, None], np.arange(tokens)[None, :]
    spread = jnp.asarray(col == (row % 10) * words + row // 10, jnp.bfloat16)
    units = (n_dp + (n_dp - 2) * (n_t // n_dp)) * SPLIT
    far = chips - 1
    bf16 = jnp.bfloat16
    dma = pltpu.SemaphoreType.DMA
    vmem = pl.BlockSpec(memory_space=pltpu.VMEM)
    anywhere = pl.BlockSpec(memory_space=pl.ANY)
    main = hidden // LATE * (LATE - TAIL)
    flops = 2 * tokens * hidden * width + 5 * total * hidden * block
    held = pl.pallas_call(
        functools.partial(exchange, n_dp, n_t),
        out_shape=tuple(pltpu.VMEM(shape, bf16) for shape in (
            (hidden, block), (block, main), (block, main), (block, total),
            (n_dp, tokens, 2 * hidden))),
        in_specs=[anywhere] * 7,
        out_specs=[vmem] * 5,
        scratch_shapes=[
            pltpu.VMEM((tokens, width), bf16),
            pltpu.VMEM((tokens, cols), bf16),
            pltpu.VMEM((tokens, hidden), bf16),
            pltpu.VMEM((tokens, hidden), bf16),
            pltpu.VMEM((words, hidden), jnp.int32),
            pltpu.VMEM((tokens, tokens), bf16),
            pltpu.VMEM((hidden, width), bf16),
            pltpu.VMEM((tokens, hidden), jnp.float32),
            pltpu.VMEM((tokens, hidden), jnp.float32),
            pltpu.VMEM((n_dp, tokens, hidden), bf16),
            pltpu.VMEM((n_dp, tokens, block), bf16),
            pltpu.VMEM((n_dp, tokens, block), bf16),
            dma((6,)), dma, dma, dma((rows, OG_SPLIT)), dma, dma((rows, OG_SPLIT)), dma, dma((rows,)),
            dma((2,)), dma((units,)), dma((2,)), dma((2,)), dma((2,)), dma, dma, dma, dma,
            dma((2, far)), dma((2, chips)), dma((far,)), dma, dma((far,)), dma((far, LATE)), dma, dma((far, LATE)),
        ],
        compiler_params=pltpu.CompilerParams(
            collective_id=0, has_side_effects=True, vmem_limit_bytes=38 * 1024 * 1024),
        cost_estimate=pl.CostEstimate(flops=flops, bytes_accessed=20_000_000, transcendentals=0),
    )(
        out_grad.reshape(tokens, cols), layer_input.reshape(tokens, cols),
        silu_gate.reshape(tokens, hidden), up_proj.reshape(tokens, hidden),
        slope_codes.reshape(words, hidden), spread, w_down,
    )
    across = jax.ShapeDtypeStruct((block, hidden), bf16)
    size = hidden // LATE
    return pl.pallas_call(
        finish,
        out_shape=(jax.ShapeDtypeStruct((hidden, block), bf16), across, across),
        in_specs=[vmem] * 5,
        out_specs=[anywhere] * 3,
        scratch_shapes=[
            pltpu.VMEM((TAIL, block, size), bf16), pltpu.VMEM((TAIL, block, size), bf16), dma((3 + 2 * TAIL,))],
        compiler_params=pltpu.CompilerParams(vmem_limit_bytes=12 * 1024 * 1024),
    )(*(pltpu.with_memory_space_constraint(value, pltpu.VMEM) for value in held))


def solution(mesh):
    n_dp, n_t = mesh.shape["dp"], mesh.shape["tensor"]
    return jax.shard_map(
        functools.partial(shards, n_dp, n_t),
        mesh=mesh,
        in_specs=(
            P(None, "dp", "tensor"),
            P(None, "dp", "tensor"),
            P("tensor", None),
            P(None, "dp", "tensor"),
            P(None, "dp", "tensor"),
            P(None, "dp", "tensor"),
        ),
        out_specs=(P("tensor", "dp"), P("dp", "tensor"), P("dp", "tensor")),
        check_vma=False,
    )
```

time: 62.9 us -> 58.2 us (0.925)
  Pallas kernels: 62.1 us -> 57.2 us
    pallas_call x1, Pallas kernels: 57.5 us -> 52.7 us  [shards(): pl.pallas_call(functools.partial(exchange, n_dp, n_t), out_shape=tuple((p...]
where the time goes in v3:
time: 58.2 us; the launch traced here: 57.9 us
  Pallas kernels  57.2 us (98%)
  between operations  0.64 us (1%)
    pallas_call x1, Pallas kernels, shards(): pl.pallas_call(functools.partial(exchange, n_dp, n_t), out_shape=tuple((p...  52.7 us
    pallas_call x1, Pallas kernels, shards(): pl.pallas_call(finish, out_shape=(jax.ShapeDtypeStruct((hidden, block), b...  4.59 us

profile of v3, /device:TPU:0, one launch (start us, length us, event | category | flops | bytes accessed | tf_op | source)
XLA Modules:
  0.0 57.9 jit_solution(14306057502598632159)
XLA Ops:
  0.6 52.7 %shard_map.94 = (bf16[2048,1024]{1,0:T(8,128)(2,1)S(1)}, bf16[1024,1792]{1,0:T(8,128)(2,1)S(1)}, bf16[1024,1792]{1,0:T(8,128)(2,1)S(1)}, bf16[1024,640]{1,0:T(8,128)(2,1)S(1)}, bf16[4,160,4096]{2,1,0:T(8,128)(2,1)S(1)}) custom-call(bf16[160,512]{1,0:T(8,128)(2,1)} %bitcast.7, bf16[160,512]{1,0:T(8,128)(2,1)} %bitcast.8, bf16[160,2048]{1,0:T(8,128)(2,1)} %bitcast.5, ...), custom_call_target="tpu_custom_call" | custom-call | flops 9395240960 | bytes 20000000 | tf_op jit(solution)/shard_map/pallas_call | solution.py:688
  53.3 4.6 %shard_map.95 = (bf16[2048,1024]{1,0:T(8,128)(2,1)}, bf16[1024,2048]{1,0:T(8,128)(2,1)}, bf16[1024,2048]{1,0:T(8,128)(2,1)}) custom-call(bf16[2048,1024]{1,0:T(8,128)(2,1)S(1)} %get-tuple-element.8.down_in, bf16[1024,1792]{1,0:T(8,128)(2,1)S(1)} %get-tuple-element.9.gate_in, bf16[1024,1792]{1,0:T(8,128)(2,1)S(1)} %get-tuple-element.10.up_in, ...), custom_call_target="tpu_custom_call" | custom-call | tf_op jit(solution)/shard_map/pallas_call | solution.py:722

commit v4 on v3

--- a/solution.py
+++ b/solution.py
@@ -13,7 +13,7 @@
 EARLY = 4
 HELD = 1
 LATE = 8
-DOWN_AT = 4
+DOWN_AT = 5
 RELAY_AT = 9
 THEN = 3
 AHEAD = 1
@@ -32,7 +32,7 @@
 def exchange(n_dp, n_t, out_hbm, in_hbm, silu_hbm, up_hbm, code_hbm, spread_hbm, w_hbm,
              down, gate_main, up_main, turned, both_all,
              og, li, silu, up, codes, spread, w, slopes_up, acc, hid_all, xin, xout,
-             l_sem, w_sem, u_send, u_recv, d_send, d_recv, y_send, y_recv,
+             l_sem, w_sem, u_send, d_send, r_recv, y_send, y_recv,
              x_send, c_recv, zu_send, zd_send, cy_send, cy_recv, o_sem, o_send, o_recv,
              ax_send, ac_send, hx_recv, hc_recv, hp_recv, ax_recv, ac_recv, ap_recv):
     chips = n_dp // 2
@@ -126,21 +126,21 @@
     def og_piece(row, col, h):
         return og.at[:, span((row * 2 + col) * fine + h, cols // fine)]
 
+    def along(row, h, send, tensor):
+        piece = og_piece(row, y, h)
+        return remote(piece, piece, send, r_recv.at[row, h], d, tensor)
+
     def up_copy(s, h):
-        piece = og_piece(lax.max(z - s + 1, 0), y, h)
-        return remote(piece, piece, u_send, u_recv.at[s - 1, h], d, z_up)
+        return along(lax.max(z - s + 1, 0), h, u_send, z_up)
 
     def down_copy(s, h):
-        piece = og_piece(lax.min(z + s - 1, rows - 1), y, h)
-        return remote(piece, piece, d_send, d_recv.at[s - 1, h], d, z_down)
+        return along(lax.min(z + s - 1, rows - 1), h, d_send, z_down)
 
     def up_wait(s, h):
-        piece = og_piece(lax.max(z - s, 0), y, h)
-        return remote(piece, piece, u_send, u_recv.at[s - 1, h], d, z_up)
+        return along(lax.max(z - s, 0), h, u_send, z_up)
 
     def down_wait(s, h):
-        piece = og_piece(lax.min(z + s, rows - 1), y, h)
-        return remote(piece, piece, d_send, d_recv.at[s - 1, h], d, z_down)
+        return along(lax.min(z + s, rows - 1), h, d_send, z_down)
 
     def across(row, h):
         piece = og_piece(row, y, h)
@@ -448,23 +448,23 @@
             for j in range(EARLY - HELD, EARLY):
                 send_own(0, j)
 
-        @pl.when(jnp.logical_and(last_part, at_in_head))
-        def _():
-            @pl.when(s == 1)
+        @pl.when(at_in_head)
+        def _():
+            @pl.when(e == fine - 1)
             def _():
                 lax.fori_loop(near, n_in, head_wait, 0)
 
-            @pl.when(jnp.logical_and(in_up, s == lax.max(z, 1)))
+            @pl.when(jnp.logical_and(in_up, e == fine * lax.max(z, 1) - 1))
             def _():
                 lax.fori_loop(jnp.where(z == 0, near, 0), n_in, head_up, 0)
 
-            @pl.when(jnp.logical_and(in_down, s == lax.max(rows - 1 - z, 1)))
+            @pl.when(jnp.logical_and(in_down, e == fine * lax.max(rows - 1 - z, 1) - 1))
             def _():
                 lax.fori_loop(jnp.where(z == rows - 1, near, 0), n_in, head_down, 0)
 
-        @pl.when(jnp.logical_and(jnp.logical_and(s == rows - 1, last_part), at_in_head))
-        def _():
-            lax.fori_loop(0, n_in, in_side, 0)
+            @pl.when(e == arrivals - 1)
+            def _():
+                lax.fori_loop(0, n_in, in_side, 0)
 
         @pl.when(e == fine - 1)
         def _():
@@ -705,7 +705,7 @@
             pltpu.VMEM((n_dp, tokens, hidden), bf16),
             pltpu.VMEM((n_dp, tokens, block), bf16),
             pltpu.VMEM((n_dp, tokens, block), bf16),
-            dma((6,)), dma, dma, dma((rows, OG_SPLIT)), dma, dma((rows, OG_SPLIT)), dma, dma((rows,)),
+            dma((6,)), dma, dma, dma, dma((rows, OG_SPLIT)), dma, dma((rows,)),
             dma((2,)), dma((units,)), dma((2,)), dma((2,)), dma((2,)), dma, dma, dma, dma,
             dma((2, far)), dma((2, chips)), dma((far,)), dma, dma((far,)), dma((far, LATE)), dma, dma((far, LATE)),
         ],

time: 58.2 us -> 58 us (level)
  no operation moved by 1% of the time
where the time goes in v4:
time: 58 us; the launch traced here: 57.7 us
  Pallas kernels  57.1 us (98%)
  between operations  0.64 us (1%)
    pallas_call x1, Pallas kernels, shards(): pl.pallas_call(functools.partial(exchange, n_dp, n_t), out_shape=tuple((p...  52.5 us
    pallas_call x1, Pallas kernels, shards(): pl.pallas_call(finish, out_shape=(jax.ShapeDtypeStruct((hidden, block), b...  4.59 us

profile of v4, /device:TPU:0, one launch (start us, length us, event | category | flops | bytes accessed | tf_op | source)
XLA Modules:
  0.0 57.7 jit_solution(10242495815927392921)
XLA Ops:
  0.6 52.5 %shard_map.94 = (bf16[2048,1024]{1,0:T(8,128)(2,1)S(1)}, bf16[1024,1792]{1,0:T(8,128)(2,1)S(1)}, bf16[1024,1792]{1,0:T(8,128)(2,1)S(1)}, bf16[1024,640]{1,0:T(8,128)(2,1)S(1)}, bf16[4,160,4096]{2,1,0:T(8,128)(2,1)S(1)}) custom-call(bf16[160,512]{1,0:T(8,128)(2,1)} %bitcast.7, bf16[160,512]{1,0:T(8,128)(2,1)} %bitcast.8, bf16[160,2048]{1,0:T(8,128)(2,1)} %bitcast.5, ...), custom_call_target="tpu_custom_call" | custom-call | flops 9395240960 | bytes 20000000 | tf_op jit(solution)/shard_map/pallas_call | solution.py:688
  53.1 4.6 %shard_map.95 = (bf16[2048,1024]{1,0:T(8,128)(2,1)}, bf16[1024,2048]{1,0:T(8,128)(2,1)}, bf16[1024,2048]{1,0:T(8,128)(2,1)}) custom-call(bf16[2048,1024]{1,0:T(8,128)(2,1)S(1)} %get-tuple-element.8.down_in, bf16[1024,1792]{1,0:T(8,128)(2,1)S(1)} %get-tuple-element.9.gate_in, bf16[1024,1792]{1,0:T(8,128)(2,1)S(1)} %get-tuple-element.10.up_in, ...), custom_call_target="tpu_custom_call" | custom-call | tf_op jit(solution)/shard_map/pallas_call | solution.py:722

commit v5 on v4

--- a/solution.py
+++ b/solution.py
@@ -14,7 +14,7 @@
 HELD = 1
 LATE = 8
 DOWN_AT = 5
-RELAY_AT = 9
+RELAY_AT = 7
 THEN = 3
 AHEAD = 1
 TAIL = 1
@@ -26,7 +26,7 @@
 OUT_PACE = 2
 OUT_HOP = 2
 WAVE_AT = 0
-LAG = 5
+LAG = 4
 
 
 def exchange(n_dp, n_t, out_hbm, in_hbm, silu_hbm, up_hbm, code_hbm, spread_hbm, w_hbm,

time: 58 us -> 58 us (level)
  no operation moved by 1% of the time
where the time goes in v5:
time: 58 us; the launch traced here: 57.7 us
  Pallas kernels  57.1 us (98%)
  between operations  0.64 us (1%)
    pallas_call x1, Pallas kernels, shards(): pl.pallas_call(functools.partial(exchange, n_dp, n_t), out_shape=tuple((p...  52.5 us
    pallas_call x1, Pallas kernels, shards(): pl.pallas_call(finish, out_shape=(jax.ShapeDtypeStruct((hidden, block), b...  4.59 us

profile of v5, /device:TPU:0, one launch (start us, length us, event | category | flops | bytes accessed | tf_op | source)
XLA Modules:
  0.0 57.7 jit_solution(14835175880241836444)
XLA Ops:
  0.6 52.5 %shard_map.94 = (bf16[2048,1024]{1,0:T(8,128)(2,1)S(1)}, bf16[1024,1792]{1,0:T(8,128)(2,1)S(1)}, bf16[1024,1792]{1,0:T(8,128)(2,1)S(1)}, bf16[1024,640]{1,0:T(8,128)(2,1)S(1)}, bf16[4,160,4096]{2,1,0:T(8,128)(2,1)S(1)}) custom-call(bf16[160,512]{1,0:T(8,128)(2,1)} %bitcast.7, bf16[160,512]{1,0:T(8,128)(2,1)} %bitcast.8, bf16[160,2048]{1,0:T(8,128)(2,1)} %bitcast.5, ...), custom_call_target="tpu_custom_call" | custom-call | flops 9395240960 | bytes 20000000 | tf_op jit(solution)/shard_map/pallas_call | solution.py:688
  53.1 4.6 %shard_map.95 = (bf16[2048,1024]{1,0:T(8,128)(2,1)}, bf16[1024,2048]{1,0:T(8,128)(2,1)}, bf16[1024,2048]{1,0:T(8,128)(2,1)}) custom-call(bf16[2048,1024]{1,0:T(8,128)(2,1)S(1)} %get-tuple-element.8.down_in, bf16[1024,1792]{1,0:T(8,128)(2,1)S(1)} %get-tuple-element.9.gate_in, bf16[1024,1792]{1,0:T(8,128)(2,1)S(1)} %get-tuple-element.10.up_in, ...), custom_call_target="tpu_custom_call" | custom-call | tf_op jit(solution)/shard_map/pallas_call | solution.py:722
